TPU v7x, 8 devices: a whole 2x2x1 slice. The times are simulated.
8 devices in a mesh: dp: 2 (over z, y), tp: 4 (over x, core).
Axes of the slice: x: 2, y: 2, z: 1, core: 2. Of those that a mesh axis runs over, the one named last changes fastest.
Arguments:
- irreps: bfloat16 [256, 25, 128], P('dp', None, 'tp')
- norm_gain: float32 [5, 128], P(None, 'tp')
- w_up: bfloat16 [5, 128, 512], P(None, None, 'tp')
- w_gate: bfloat16 [128, 512], P(None, 'tp')
- w_down: bfloat16 [5, 512, 128], P(None, 'tp')
- to_grid: float32 [25, 324], replicated
- from_grid: float32 [324, 24], replicated
- grad_out: bfloat16 [256, 25, 128], P('dp', None, 'tp')
Outputs:
- output 1: bfloat16 [256, 25, 128], P('dp', None, 'tp')
- output 2: bfloat16 [256, 25, 128], P('dp', None, 'tp')
- output 3: bfloat16 [5, 128, 512], P(None, None, 'tp')
- output 4: bfloat16 [128, 512], P(None, 'tp')
- output 5: bfloat16 [5, 512, 128], P(None, 'tp')
All inputs are finite; a program needn't handle non-finite values.
Results may differ from a plain program's by a relative error of at most 0.0125651.
Values are sent between devices in bfloat16 or wider.
A program may use at most 1 GiB of HBM per device.

v0:
```python
import math
import jax
import jax.numpy as jnp
from jax import lax
from jax.sharding import PartitionSpec as P

NORM_EPS = 1e-5


def expand_rows(per_degree):
    return jnp.concatenate([jnp.broadcast_to(per_degree[degree:degree + 1], (2 * degree + 1,) + per_degree.shape[1:]) for degree in range(per_degree.shape[0])], axis=0)


def degree_sums(per_coef):
    degrees = math.isqrt(per_coef.shape[0])
    return jnp.stack([per_coef[degree * degree:(degree + 1) * (degree + 1)].sum(axis=0) for degree in range(degrees)], axis=0)


def silu_grad(pre_act):
    sig_val = jax.nn.sigmoid(pre_act)
    return sig_val * (1.0 + pre_act * (1.0 - sig_val))


def hidden_block(xn_blk, grad_blk, up_rows, gate_loc, down_rows, grid_in, grid_back):
    hidden_act = jnp.einsum('nkc,kch->nkh', xn_blk, up_rows, preferred_element_type=jnp.float32).astype(jnp.bfloat16)
    pre_gate = jnp.dot(xn_blk[:, 0, :], gate_loc, preferred_element_type=jnp.float32).astype(jnp.bfloat16)
    gate_pre_f = pre_gate.astype(jnp.float32)
    gate_val = jax.nn.silu(gate_pre_f).astype(jnp.bfloat16)
    pre_grid = jnp.einsum('nkh,kg->ngh', hidden_act, grid_in, preferred_element_type=jnp.float32).astype(jnp.bfloat16)
    grid_pre_f = pre_grid.astype(jnp.float32)
    grid_val = jax.nn.silu(grid_pre_f).astype(jnp.bfloat16)
    back_proj = jnp.einsum('ngh,gk->nkh', grid_val, grid_back, preferred_element_type=jnp.float32).astype(jnp.bfloat16)
    mixed_act = jnp.concatenate([gate_val[:, None, :], back_proj], axis=1)
    part_out = jnp.einsum('nkh,khc->nkc', mixed_act, down_rows, preferred_element_type=jnp.float32).astype(jnp.bfloat16)
    d_mixed = jnp.einsum('nkc,khc->nkh', grad_blk, down_rows, preferred_element_type=jnp.float32).astype(jnp.bfloat16)
    g_down = jnp.einsum('nkh,nkc->khc', mixed_act, grad_blk, preferred_element_type=jnp.float32)
    d_grid = jnp.einsum('nkh,gk->ngh', d_mixed[:, 1:, :], grid_back, preferred_element_type=jnp.float32).astype(jnp.bfloat16)
    d_pre_grid = (d_grid.astype(jnp.float32) * silu_grad(grid_pre_f)).astype(jnp.bfloat16)
    d_hidden = jnp.einsum('ngh,kg->nkh', d_pre_grid, grid_in, preferred_element_type=jnp.float32).astype(jnp.bfloat16)
    d_pre_gate = (d_mixed[:, 0, :].astype(jnp.float32) * silu_grad(gate_pre_f)).astype(jnp.bfloat16)
    g_up = jnp.einsum('nkc,nkh->kch', xn_blk, d_hidden, preferred_element_type=jnp.float32)
    g_gate = jnp.einsum('nc,nh->ch', xn_blk[:, 0, :], d_pre_gate, preferred_element_type=jnp.float32)
    d_xn = jnp.einsum('nkh,kch->nkc', d_hidden, up_rows, preferred_element_type=jnp.float32)
    d_xn_zero = d_xn[:, 0, :] + jnp.einsum('nh,ch->nc', d_pre_gate, gate_loc, preferred_element_type=jnp.float32)
    d_xn = jnp.concatenate([d_xn_zero[:, None, :], d_xn[:, 1:, :]], axis=1).astype(jnp.bfloat16)
    return part_out, d_xn, g_up, g_gate, g_down


def hidden_pass(xn_full, grad_full, up_loc, gate_loc, down_loc, to_grid, from_grid):
    node_count, coef_count, channels = xn_full.shape
    blk_rows = math.gcd(node_count, 128)
    blk_count = node_count // blk_rows
    up_rows = expand_rows(up_loc)
    down_rows = expand_rows(down_loc)
    grid_in = to_grid.astype(jnp.bfloat16)
    grid_back = from_grid.astype(jnp.bfloat16)

    def scan_step(grad_sums, blk_pair):
        part_out, d_xn, g_up, g_gate, g_down = hidden_block(blk_pair[0], blk_pair[1], up_rows, gate_loc, down_rows, grid_in, grid_back)
        return (grad_sums[0] + g_up, grad_sums[1] + g_gate, grad_sums[2] + g_down), (part_out, d_xn)

    init_sums = (jnp.zeros(up_rows.shape, jnp.float32), jnp.zeros(gate_loc.shape, jnp.float32), jnp.zeros(down_rows.shape, jnp.float32))
    blk_shape = (blk_count, blk_rows, coef_count, channels)
    total_sums, (part_outs, d_xns) = lax.scan(scan_step, init_sums, (xn_full.reshape(blk_shape), grad_full.reshape(blk_shape)))
    full_shape = (node_count, coef_count, channels)
    return part_outs.reshape(full_shape), d_xns.reshape(full_shape), degree_sums(total_sums[0]), total_sums[1], degree_sums(total_sums[2])


def solution(mesh):
    tp_size = mesh.shape['tp']
    act_spec = P('dp', None, 'tp')
    in_specs = (act_spec, P(None, 'tp'), P(None, None, 'tp'), P(None, 'tp'), P(None, 'tp', None), P(None, None), P(None, None), act_spec)
    out_specs = (act_spec, act_spec, P(None, None, 'tp'), P(None, 'tp'), P(None, 'tp', None))

    def local_step(x_loc, gain_loc, up_loc, gate_loc, down_loc, to_grid, from_grid, grad_loc):
        coef_count = x_loc.shape[1]
        channels = x_loc.shape[2] * tp_size
        vec_count = channels * (coef_count - 1)
        x_f = x_loc.astype(jnp.float32)
        scalar = x_f[:, 0, :]
        vector = x_f[:, 1:, :]
        node_stats = jnp.stack([jnp.sum(scalar, axis=-1), jnp.sum(scalar * scalar, axis=-1), jnp.sum(vector * vector, axis=(1, 2))], axis=-1)
        node_stats = lax.psum(node_stats, 'tp')
        mean_s = node_stats[:, 0:1] / channels
        inv_s = lax.rsqrt(node_stats[:, 1:2] / channels - mean_s * mean_s + NORM_EPS)
        inv_v = lax.rsqrt(node_stats[:, 2] / vec_count + NORM_EPS)[:, None, None]
        hat_s = (scalar - mean_s) * inv_s
        hat_v = vector * inv_v
        gain_rows = expand_rows(gain_loc)
        xn_loc = jnp.concatenate([(hat_s * gain_rows[0])[:, None, :], hat_v * gain_rows[1:]], axis=1).astype(jnp.bfloat16)
        xn_full = lax.all_gather(xn_loc, 'tp', axis=2, tiled=True)
        grad_full = lax.all_gather(grad_loc, 'tp', axis=2, tiled=True)
        part_out, d_xn_part, g_up, g_gate, g_down = hidden_pass(xn_full, grad_full, up_loc, gate_loc, down_loc, to_grid, from_grid)
        ffn_delta = lax.psum_scatter(part_out, 'tp', scatter_dimension=2, tiled=True)
        out_loc = (x_f + ffn_delta.astype(jnp.float32)).astype(jnp.bfloat16)
        d_norm = lax.psum_scatter(d_xn_part, 'tp', scatter_dimension=2, tiled=True).astype(jnp.float32)
        d_hat_s = d_norm[:, 0, :] * gain_rows[0]
        d_hat_v = d_norm[:, 1:, :] * gain_rows[1:]
        back_stats = jnp.stack([jnp.sum(d_hat_s, axis=-1), jnp.sum(d_hat_s * hat_s, axis=-1), jnp.sum(d_hat_v * vector, axis=(1, 2))], axis=-1)
        back_stats = lax.psum(back_stats, 'tp')
        dx_s = inv_s * (d_hat_s - back_stats[:, 0:1] / channels - hat_s * back_stats[:, 1:2] / channels)
        dx_v = inv_v * d_hat_v - vector * (inv_v ** 3) * (back_stats[:, 2] / vec_count)[:, None, None]
        d_irreps = (jnp.concatenate([dx_s[:, None, :], dx_v], axis=1) + grad_loc.astype(jnp.float32)).astype(jnp.bfloat16)
        d_up = lax.psum(g_up, 'dp').astype(jnp.bfloat16)
        d_gate = lax.psum(g_gate, 'dp').astype(jnp.bfloat16)
        d_down = lax.psum(g_down, 'dp').astype(jnp.bfloat16)
        return out_loc, d_irreps, d_up, d_gate, d_down

    return jax.shard_map(local_step, mesh=mesh, in_specs=in_specs, out_specs=out_specs, check_vma=False)
```

profile of v0, /device:TPU:0, one launch (start us, length us, event | category | flops | bytes accessed | tf_op | source)
XLA Modules:
  0.0 129.6 jit_solution(605931821900757373)
XLA Ops:
  7.2 0.0 copy-start
  7.2 0.0 copy-start.7
  7.2 0.0 reduce-scatter.5.cloned.1.call-start
  7.2 1.0 convert_element_type.127
  8.2 0.1 multiply_reduce_fusion.1
  8.4 8.7 %psum.35 = f32[128,3]{0,1:T(4,128)S(1)} all-reduce(f32[128,3]{0,1:T(4,128)S(1)} %pad_maximum_fusion.4), channel_id=1, replica_groups=mesh['dp'=2,'tp'=4] {'tp'}, use_global_device_ids=true, to_apply=%region_3.0 | all-reduce | flops 384 | bytes 3072 | tf_op jit(solution)/shard_map/psum | solution.py:83
  17.2 0.9 slice_bitcast_fusion.18
  18.0 0.8 slice_bitcast_fusion.7
  18.9 0.1 copy.17
  19.0 0.1 copy.15
  19.1 0.1 copy.14
  19.2 0.1 copy.31
  19.4 0.1 copy.16
  19.6 0.2 multiply_convert_fusion
  19.7 0.1 multiply_convert_fusion.2
  19.8 11.7 %all_gather.6 = bf16[128,25,128]{0,2,1:T(8,128)(2,1)S(1)} all-gather(bf16[128,25,32]{0,2,1:T(8,128)(2,1)S(1)} %pad_maximum_fusion.2), channel_id=1, replica_groups=mesh['dp'=2,'tp'=4] {'tp'}, dimensions={2}, use_global_device_ids=true | all-gather | bytes 1024000 | tf_op jit(solution)/shard_map/all_gather | solution.py:91
  31.5 10.9 %all_gather.7 = bf16[128,25,128]{0,2,1:T(8,128)(2,1)S(1)} all-gather(bf16[128,25,32]{0,2,1:T(8,128)(2,1)} %param.15), channel_id=1, replica_groups=mesh['dp'=2,'tp'=4] {'tp'}, dimensions={2}, use_global_device_ids=true | all-gather | bytes 1024000 | tf_op jit(solution)/shard_map/all_gather | solution.py:92
  42.5 0.1 broadcast_dynamic-update-slice_fusion.3
  42.6 0.1 broadcast_dynamic-update-slice_fusion.1
  42.6 0.0 copy-start.3
  42.7 0.0 copy-start.8
  42.7 0.5 fusion.23
  43.1 0.0 copy-start.4
  43.1 1.1 slice.179
  44.2 0.8 slice_bitcast_fusion.3
  45.0 0.0 copy-done
  45.1 0.2 fusion.28
  45.3 0.1 broadcast_dynamic-update-slice_fusion.2
  45.4 0.1 broadcast_dynamic-update-slice_fusion
  45.5 0.0 copy-done.3
  45.5 0.0 copy-done.4
  45.5 0.0 copy-start.1
  45.5 0.9 copy-done.1
  46.4 1.4 %fusion.61 = bf16[25,128,128]{2,1,0:T(8,128)(2,1)} fusion(bf16[25,128,128]{2,1,0:T(8,128)(2,1)S(1)} %broadcast_dynamic-update-slice_fusion, bf16[128,25,128]{0,2,1:T(8,128)(2,1)S(1)} %all_gather.6), kind=kOutput, calls=%fused_computation.130 | convolution fusion | flops 104857600 | bytes 2457600 | tf_op jit(solution)/shard_map/while/body/eval_jaxpr/nkc,kch->nkh/dot_general | solution.py:25
  47.7 1.9 %copy.26 = bf16[25,128,128]{1,0,2:T(8,128)(2,1)S(1)} copy(bf16[25,128,128]{2,1,0:T(8,128)(2,1)} %fusion.61) | data formatting | bytes 1638400 | tf_op jit(solution)/shard_map/while/body/eval_jaxpr/nkc,kch->nkh/dot_general | solution.py:25
  49.6 0.0 copy-done.7
  49.7 5.7 %convolution_convert_fusion = bf16[128,128,324]{1,2,0:T(8,128)(2,1)} fusion(bf16[25,128,128]{1,0,2:T(8,128)(2,1)S(1)} %copy.26, f32[25,324]{1,0:T(8,128)S(1)} %copy-done.7), kind=kOutput, calls=%fused_computation.13 | convolution fusion | flops 270737312 | bytes 11468432 | tf_op jit(solution)/shard_map/while/body/eval_jaxpr/nkh,kg->ngh/dot_general | solution.py:29
  55.3 0.0 copy-done.8
  55.3 15.8 %fusion.19 = bf16[128,25,128]{2,1,0:T(8,128)(2,1)} fusion(bf16[128,128,324]{1,2,0:T(8,128)(2,1)} %convolution_convert_fusion, bf16[128,24,128]{2,0,1:T(8,128)(2,1)} %slice.179, f32[25,324]{1,0:T(8,128)S(1)} %copy-done.7, f32[324,24]{0,1:T(8,128)S(1)} %copy-done.8), kind=kOutput, calls=%fused_computation.21 | convolution fusion | flops 584351232 | bytes 12285968 | tf_op jit(solution)/shard_map/while/body/eval_jaxpr/ngh,kg->nkh/dot_general | solution.py:39
  71.2 1.9 %convolution_bitcast_fusion = f32[128,25,128]{0,2,1:T(8,128)S(1)} fusion(bf16[25,128,128]{2,1,0:T(8,128)(2,1)S(1)} %copy-done.2, bf16[128,25,128]{2,1,0:T(8,128)(2,1)} %fusion.19), kind=kOutput, calls=%fused_computation.16 | convolution fusion | flops 104857600 | bytes 3276800 | tf_op jit(solution)/shard_map/while/body/eval_jaxpr/nkh,kch->nkc/dot_general | solution.py:43
  73.1 0.1 slice.258
  73.2 0.9 fusion.29
  74.2 1.0 pad_maximum_fusion.1
  75.1 0.0 reduce-scatter.5.cloned.1.call-update
  75.2 0.0 reduce-scatter.3.cloned.1.call-start
  75.2 8.6 %fusion.24 = bf16[128,24,128]{2,1,0:T(8,128)(2,1)S(1)} fusion(bf16[128,128,324]{1,2,0:T(8,128)(2,1)} %convolution_convert_fusion, f32[324,24]{0,1:T(8,128)S(1)} %copy-done.8), kind=kOutput, calls=%fused_computation.24 | convolution fusion | flops 287055456 | bytes 11434368 | tf_op jit(solution)/shard_map/while/body/eval_jaxpr/ngh,gk->nkh/dot_general | solution.py:32
  83.8 0.1 copy.18
  83.9 0.0 copy-start.6
  83.9 1.5 %pad_maximum_fusion = bf16[128,25,128]{2,1,0:T(8,128)(2,1)} fusion(bf16[128,24,128]{2,1,0:T(8,128)(2,1)S(1)} %fusion.24, bf16[128,1,128]{2,1,0:T(2,128)(2,1)S(1)} %copy.18), kind=kLoop, calls=%fused_computation.30 | loop fusion | flops 1638400 | bytes 1638400 | tf_op jit(solution)/shard_map/while/body/eval_jaxpr/concatenate | solution.py:33
  85.3 2.2 %copy.25 = bf16[128,25,128]{0,2,1:T(8,128)(2,1)S(1)} copy(bf16[128,25,128]{2,1,0:T(8,128)(2,1)} %pad_maximum_fusion) | data formatting | bytes 1638400 | tf_op jit(solution)/shard_map/while/body/eval_jaxpr/concatenate | solution.py:33
  87.5 2.4 %fusion.22 = bf16[128,25,128]{0,2,1:T(8,128)(2,1)} fusion(bf16[25,128,128]{1,2,0:T(8,128)(2,1)} %copy-done.3, bf16[128,25,128]{0,2,1:T(8,128)(2,1)S(1)} %copy.25), kind=kOutput, calls=%fused_computation.22 | convolution fusion | flops 105267200 | bytes 2457600 | tf_op jit(solution)/shard_map/while/body/eval_jaxpr/nkh,khc->nkc/dot_general | solution.py:34
  89.9 0.0 reduce-scatter.3.cloned.1.call-update
  90.0 0.9 fusion.40
  90.9 0.7 fusion.62
  91.7 1.9 %fusion.34 = f32[25,128,128]{2,1,0:T(8,128)S(1)} fusion(bf16[128,25,128]{0,2,1:T(8,128)(2,1)S(1)} %all_gather.6, bf16[128,25,128]{2,1,0:T(8,128)(2,1)} %fusion.19), kind=kOutput, calls=%fused_computation.35 | convolution fusion | flops 104857600 | bytes 3276800 | tf_op jit(solution)/shard_map/while/body/eval_jaxpr/nkc,nkh->kch/dot_general | solution.py:41
  93.8 19.4 %all-reduce.2 = (bf16[5,128,128]{2,1,0:T(8,128)(2,1)}, bf16[128,128]{1,0:T(8,128)(2,1)}, bf16[5,128,128]{2,1,0:T(8,128)(2,1)}) all-reduce(f32[5,128,128]{2,1,0:T(8,128)S(1)} %get-tuple-element.72, f32[128,128]{1,0:T(8,128)S(1)} %fusion.40, f32[5,128,128]{2,1,0:T(8,128)S(1)} %get-tuple-element.71), channel_id=1, replica_groups=mesh['dp'=2,'tp'=4] {'dp'}, use_global_device_ids=true, to_apply=%region_14.15 | all-reduce | flops 180224 | bytes 1081344 | tf_op jit(solution)/shard_map/psum | solution.py:104
  113.2 1.0 convert_element_type.156
  114.2 0.1 fusion.50
  114.2 0.2 multiply_reduce_fusion
  114.4 5.7 %psum.36 = f32[128,3]{0,1:T(4,128)S(1)} all-reduce(f32[128,3]{0,1:T(4,128)S(1)} %pad_maximum_fusion.5), channel_id=1, replica_groups=mesh['dp'=2,'tp'=4] {'tp'}, use_global_device_ids=true, to_apply=%region_9.10 | all-reduce | flops 384 | bytes 3072 | tf_op jit(solution)/shard_map/psum | solution.py:100
  120.1 0.1 subtract_multiply_fusion
  120.2 0.2 multiply_subtract_fusion
  120.4 0.7 fusion.37
  121.1 1.7 %add_convert_fusion = bf16[128,25,32]{0,2,1:T(8,128)(2,1)} fusion(bf16[128,25,32]{0,2,1:T(8,128)(2,1)} %reduce-scatter.3.cloned.1.call-done, bf16[128,25,32]{0,2,1:T(8,128)(2,1)S(1)} %copy-done.5), kind=kLoop, calls=%fused_computation.44 | loop fusion | flops 409600 | bytes 614400 | tf_op jit(solution)/shard_map/convert_element_type | solution.py:95
  (43 shorter events, 0.6 us)
Async XLA Ops:
  7.2 37.9 %copy-start = (bf16[128,128]{1,0:T(8,128)(2,1)S(1)}, bf16[128,128]{1,0:T(8,128)(2,1)}, u32[]{:S(2)}) copy-start(bf16[128,128]{1,0:T(8,128)(2,1)} %param.11) | copy-start | bytes 98308
  7.2 42.5 %copy-start.7 = (f32[25,324]{1,0:T(8,128)S(1)}, f32[25,324]{1,0:T(8,128)}, u32[]{:S(2)}) copy-start(f32[25,324]{1,0:T(8,128)} %param.13) | copy-start | bytes 97204
  7.2 106.0 %reduce-scatter.5.cloned.1.call-start = ((), (), s32[]{:S(2)}) async-start(), calls=%async_computation.3 | async-start | bytes 1024000 | tf_op jit(solution)/shard_map/reduce_scatter | solution.py:96
  42.6 2.8 %copy-start.3 = (bf16[25,128,128]{1,2,0:T(8,128)(2,1)}, bf16[25,128,128]{1,2,0:T(8,128)(2,1)S(1)}, u32[]{:S(2)}) copy-start(bf16[25,128,128]{1,2,0:T(8,128)(2,1)S(1)} %broadcast_dynamic-update-slice_fusion.1) | copy-start | bytes 2457604
  42.7 12.7 %copy-start.8 = (f32[324,24]{0,1:T(8,128)S(1)}, f32[324,24]{0,1:T(8,128)}, u32[]{:S(2)}) copy-start(f32[324,24]{0,1:T(8,128)} %param.14) | copy-start | bytes 93316
  43.1 2.3 %copy-start.4 = (bf16[128,25,128]{2,0,1:T(8,128)(2,1)}, bf16[128,25,128]{2,0,1:T(8,128)(2,1)S(1)}, u32[]{:S(2)}) copy-start(bf16[128,25,128]{2,0,1:T(8,128)(2,1)S(1)} %fusion.23) | copy-start | bytes 2457604
  45.5 0.9 copy-start.1
  55.3 15.8 %copy-start.2 = (bf16[25,128,128]{2,1,0:T(8,128)(2,1)S(1)}, bf16[25,128,128]{2,1,0:T(8,128)(2,1)}, u32[]{:S(2)}) copy-start(bf16[25,128,128]{2,1,0:T(8,128)(2,1)} %copy-done.1) | copy-start | bytes 2457604
  75.2 46.0 %reduce-scatter.3.cloned.1.call-start = ((), (), s32[]{:S(2)}) async-start(), calls=%async_computation.2 | async-start | bytes 1024000 | tf_op jit(solution)/shard_map/reduce_scatter | solution.py:94
  83.9 36.5 %copy-start.6 = (bf16[128,25,32]{0,2,1:T(8,128)(2,1)S(1)}, bf16[128,25,32]{0,2,1:T(8,128)(2,1)}, u32[]{:S(2)}) copy-start(bf16[128,25,32]{0,2,1:T(8,128)(2,1)} %param.15) | copy-start | bytes 614404
  85.3 35.8 %copy-start.5 = (bf16[128,25,32]{0,2,1:T(8,128)(2,1)S(1)}, bf16[128,25,32]{0,2,1:T(8,128)(2,1)}, u32[]{:S(2)}) copy-start(bf16[128,25,32]{0,2,1:T(8,128)(2,1)} %param.8) | copy-start | bytes 614404
Sparse Core Ops, SparseCore 0:
  75.3 17.9 reduce-scatter.4
  95.7 17.7 reduce-scatter.2
where the time goes:
time: 130 us
  blocking collectives  56.4 us (43%)
  matrix products  40.8 us (31%)
  between operations  14.5 us (11%)
  local copies, waits for them, and re-layouts  9.89 us (8%)
  other arithmetic  7.97 us (6%)
    psum x1, blocking collectives, local_step(): d_up = lax.psum(g_up, 'dp').astype(jnp.bfloat16)  19.4 us
    dot_general x1, matrix products, hidden_block(): jnp.einsum('ngh,kg->nkh', d_pre_grid, grid_in, preferred_element_type=jnp...  15.8 us
    all_gather x1, blocking collectives, local_step(): xn_full = lax.all_gather(xn_loc, 'tp', axis=2, tiled=True)  11.7 us
    all_gather x1, blocking collectives, local_step(): grad_full = lax.all_gather(grad_loc, 'tp', axis=2, tiled=True)  10.9 us
    psum x1, blocking collectives, local_step(): node_stats = lax.psum(node_stats, 'tp')  8.75 us
    dot_general x1, matrix products, hidden_block(): jnp.einsum('ngh,gk->nkh', grid_val, grid_back, preferred_element_type=jnp...  8.57 us
    dot_general x1, matrix products, hidden_block(): jnp.einsum('nkh,kg->ngh', hidden_act, grid_in, preferred_element_type=jnp...  5.68 us
    psum x1, blocking collectives, local_step(): back_stats = lax.psum(back_stats, 'tp')  5.67 us
  transfers between devices with their start and end apart: 2, of which 0 were waited for; matrix products, arithmetic and copies ran while one was open for 16% of the time, Pallas kernels for 0%

commit v1 on v0

v1 whole, which is shorter than its diff:
```python
import functools
import math
import jax
import jax.numpy as jnp
from jax import lax
from jax.experimental import pallas as pl
from jax.experimental.pallas import tpu as pltpu
from jax.sharding import PartitionSpec as P

NORM_EPS = 1e-5
MESH = pl.DeviceIdType.MESH
F32 = jnp.float32
BF16 = jnp.bfloat16
COEFS = 25
KPAD = 32
YSTRIDE = 40
UNROLL = 2


def degree_of(k):
    return math.isqrt(k)


def rows_dot(a, b):
    return lax.dot_general(a, b, (((1,), (0,)), ((), ())), preferred_element_type=F32)


def lanes_dot(a, b):
    return lax.dot_general(a, b, (((1,), (1,)), ((), ())), preferred_element_type=F32)


def kernel(tp_size, grid_pts, x_hbm, gain_hbm, up_hbm, gate_hbm, down_hbm, tog_hbm, frg_hbm, g_hbm,
           out_ref, dx_ref, dup_ref, dgate_ref, ddown_ref,
           xg, gg, xn, mb, dyb, dpart, npart, ya, yb, zs, hs,
           gain_in, gain_snd, gain_all, gcol, up, gate, down, upt, gatet, downt,
           tog, frg, tt, tmat, fmat, ft, rb1, sb, rb2, nrb1, nsb, nrb2,
           st_snd, st_all, gdn, gdn_rb, gup, gup_rb, amat,
           loc_sem, snd_sem, rcv_sem):
    dp = lax.axis_index("dp")
    t = lax.axis_index("tp")
    core = lax.rem(t, 2)
    t1 = t + 1 - 2 * core
    t2 = lax.rem(t + 2, 4)
    t3 = lax.rem(t1 + 2, 4)
    odp = 1 - dp
    cl = xg.shape[1] // tp_size
    ch = xg.shape[1]
    nat = xg.shape[2]
    pp = tt.shape[0]

    def blk(i):
        return pl.ds(pl.multiple_of(i * cl, cl), cl)

    def local(src, dst, i):
        c = pltpu.make_async_copy(src, dst, loc_sem.at[i])
        c.start()
        return c

    def remote(src, dst, i, dev):
        return pltpu.make_async_remote_copy(src_ref=src, dst_ref=dst, send_sem=snd_sem.at[i], recv_sem=rcv_sem.at[i],
                                            device_id=dev, device_id_type=MESH)

    c_gain = local(gain_hbm, gain_in, 0)
    c_x = local(x_hbm, xg.at[:, blk(t), :], 1)
    c_tog = local(tog_hbm, tog, 2)
    c_frg = local(frg_hbm, frg, 3)
    c_up = local(up_hbm, up, 4)
    c_gate = local(gate_hbm, gate, 5)
    c_down = local(down_hbm, down, 6)
    c_g = local(g_hbm, gg.at[:, blk(t), :], 7)

    barrier = pltpu.get_barrier_semaphore()
    for dev in ({"tp": t1}, {"tp": t2}, {"tp": t3}, {"dp": odp}):
        pl.semaphore_signal(barrier, inc=1, device_id=dev, device_id_type=MESH)
    pl.semaphore_wait(barrier, 4)

    ksplit = ((0, 7), (7, 13), (13, 19), (19, 25))

    def gather_start(src, dst, base):
        far, near = [], None
        for j, (k0, k1) in enumerate(ksplit):
            c = remote(src.at[k0:k1], dst.at[k0:k1, blk(t), :], base + j, {"tp": t2})
            c.start()
            far.append(c)
        near = remote(src, dst.at[:, blk(t), :], base + 4, {"tp": t1})
        near.start()
        return far, near

    def gather_finish(far, near, dst, base):
        fwd = []
        for j, (k0, k1) in enumerate(ksplit):
            far[j].wait_recv()
            c = remote(dst.at[k0:k1, blk(t2), :], dst.at[k0:k1, blk(t2), :], base + 5 + j, {"tp": t1})
            c.start()
            fwd.append(c)
        near.wait_recv()
        for c in fwd:
            c.wait_recv()
        return fwd

    far_x, near_x = gather_start(x_hbm, xg, 0)

    gain_snd[...] = jnp.zeros_like(gain_snd)
    c_gain.wait()
    gain_snd[0:5, 0:cl] = gain_in[...]
    placed = pltpu.roll(gain_snd[...], t * cl, 1)
    gain_snd[...] = placed
    gsend = []
    for j, dev in enumerate((t1, t2, t3)):
        c = remote(gain_snd, gain_all.at[j], 20 + j, {"tp": dev})
        c.start()
        gsend.append(c)

    c_tog.wait()
    c_frg.wait()
    tpad = jnp.zeros((KPAD, 384), F32)
    tmat[...] = tpad.astype(BF16)
    ft[...] = tpad.astype(BF16)
    tmat[0:COEFS, 0:grid_pts] = tog[...].astype(BF16)
    frg_pad = jnp.concatenate([jnp.zeros((1, grid_pts), F32), frg[...]], axis=0)
    ft[0:COEFS, 0:grid_pts] = frg_pad.astype(BF16)
    for src, dst in ((tmat, tt), (ft, fmat)):
        wide = jnp.concatenate([src[...].astype(F32) * 0.5, jnp.zeros((128 - KPAD, 384), F32)], axis=0)
        for j in range(3):
            tr = wide[:, 128 * j:128 * (j + 1)].T
            rows = min(128, pp - 128 * j)
            dst[128 * j:128 * j + rows, :] = tr[0:rows, 0:KPAD].astype(BF16)
    c_up.wait()
    c_gate.wait()
    c_down.wait()
    for l in range(5):
        upt[l] = up[l].astype(F32).T.astype(BF16)
        downt[l] = down[l].astype(F32).T.astype(BF16)
    gatet[...] = gate[...].astype(F32).T.astype(BF16)
    ya[...] = jnp.zeros_like(ya)
    yb[...] = jnp.zeros_like(yb)
    for c in gsend:
        c.wait_recv()
    gain_full = placed + gain_all[0] + gain_all[1] + gain_all[2]
    for l in range(5):
        gcol[l] = jnp.broadcast_to(gain_full[l:l + 1, :], (ch, ch)).T

    c_x.wait()
    fwd_x = gather_finish(far_x, near_x, xg, 0)
    for c in far_x:
        c.wait_send()
    far_g, near_g = gather_start(g_hbm, gg, 10)

    x0 = xg[0].astype(F32)
    mean_s = jnp.sum(x0, axis=0, keepdims=True) / ch
    cent = x0 - mean_s
    inv_s = lax.rsqrt(jnp.sum(cent * cent, axis=0, keepdims=True) / ch + NORM_EPS)
    hat_s = cent * inv_s
    acc = jnp.zeros((ch, nat), F32)
    for k in range(1, COEFS):
        v = xg[k].astype(F32)
        acc = acc + v * v
    inv_v = lax.rsqrt(jnp.sum(acc, axis=0, keepdims=True) / (ch * (COEFS - 1)) + NORM_EPS)
    xn[0] = (hat_s * gcol[0]).astype(BF16)
    for k in range(1, COEFS):
        xn[k] = (xg[k].astype(F32) * inv_v * gcol[degree_of(k)]).astype(BF16)

    def spread(get, lhs_of):
        for l in range(5):
            k0, k1 = l * l, (l + 1) * (l + 1)
            lhs = lhs_of(l)
            for k in range(k0, k1):
                r = rows_dot(lhs, get(k))
                ya[pl.ds(k, 64, stride=YSTRIDE), :] = r[0:64]
                yb[pl.ds(k, 64, stride=YSTRIDE), :] = r[64:128]

    spread(lambda k: xn[k], lambda l: upt[l])
    a_r = rows_dot(gatet[...], xn[0]).astype(BF16)
    amat[...] = a_r
    a_h = a_r.astype(F32) * 0.5
    mb[0] = (a_h * (1.0 + jnp.tanh(a_h))).astype(BF16)

    def pair(i):
        base = pl.multiple_of(i * YSTRIDE, 8)
        return jnp.concatenate([ya[pl.ds(base, KPAD), :], yb[pl.ds(base, KPAD), :]], axis=1).astype(BF16)

    def put(i, r):
        zs[pl.ds(i, KPAD, stride=136), :] = r[:, 0:128]
        zs[pl.ds(i + 64, KPAD, stride=136), :] = r[:, 128:256]

    def fwd_body(it, carry):
        for j in range(UNROLL):
            i = it * UNROLL + j
            hb = rows_dot(tt[...], pair(i)).astype(BF16)
            hs[pl.ds(pl.multiple_of(i * pp, 16), pp), :] = hb
            h = hb.astype(F32)
            s = (h * (1.0 + jnp.tanh(h))).astype(BF16)
            put(i, rows_dot(ft[:, 0:pp], s))
        return carry

    lax.fori_loop(0, 64 // UNROLL, fwd_body, 0)

    for k in range(1, COEFS):
        mb[k] = zs[k * 136:k * 136 + 128, :].astype(BF16)
    for k in range(COEFS):
        dpart[k] = rows_dot(downt[degree_of(k)], mb[k]).astype(BF16)

    def scatter_near(part, rb, base):
        cs = []
        for j, b in enumerate((t3, t1)):
            c = remote(part.at[:, blk(b), :], rb.at[j], base + j, {"tp": t1})
            c.start()
            cs.append(c)
        return cs

    near_d = scatter_near(dpart, rb1, 23)

    fwd_g = gather_finish(far_g, near_g, gg, 10)
    c_g.wait()
    spread(lambda k: gg[k], lambda l: down[l])
    dm0 = rows_dot(down[0], gg[0]).astype(BF16).astype(F32)
    a_h = amat[...].astype(F32) * 0.5
    w_a = 1.0 + jnp.tanh(a_h)
    da = (dm0 * (0.5 * w_a * (1.0 + a_h * (2.0 - w_a)))).astype(BF16)

    near_d[0].wait_recv()
    sb[...] = (dpart[:, blk(t2), :].astype(F32) + rb1[0].astype(F32)).astype(BF16)
    for l in range(5):
        acc = jnp.zeros((128, ch), F32)
        for k in range(l * l, (l + 1) * (l + 1)):
            acc = acc + lanes_dot(mb[k], gg[k])
        gdn[l] = acc
    far_d = remote(sb, rb2, 25, {"tp": t2})
    far_d.start()
    half = 64
    mine = pl.ds(pl.multiple_of(dp * half, half), half)
    theirs = pl.ds(pl.multiple_of(odp * half, half), half)
    ex_dn = remote(gdn.at[:, theirs, :], gdn_rb, 26, {"dp": odp})
    ex_dn.start()

    def bwd_body(it, carry):
        for j in range(UNROLL):
            i = it * UNROLL + j
            dg = rows_dot(fmat[...], pair(i)).astype(BF16).astype(F32)
            h = hs[pl.ds(pl.multiple_of(i * pp, 16), pp), :].astype(F32)
            w = 1.0 + jnp.tanh(h)
            dpre = (dg * (w * (1.0 + h * (2.0 - w)))).astype(BF16)
            put(i, rows_dot(tmat[:, 0:pp], dpre))
        return carry

    lax.fori_loop(0, 64 // UNROLL, bwd_body, 0)

    for k in range(COEFS):
        dyb[k] = zs[k * 136:k * 136 + 128, :].astype(BF16)
    s3 = jnp.zeros((ch, nat), F32)
    for k in range(COEFS):
        r = rows_dot(up[degree_of(k)], dyb[k])
        if k == 0:
            r = r + rows_dot(gate[...], da)
        rb = r.astype(BF16)
        npart[k] = rb
        rf = rb.astype(F32) * gcol[degree_of(k)]
        if k == 0:
            st0 = jnp.sum(rf, axis=0, keepdims=True)
            st1 = jnp.sum(rf * hat_s, axis=0, keepdims=True)
        else:
            s3 = s3 + rf * xg[k].astype(F32)
    st2 = jnp.sum(s3, axis=0, keepdims=True)
    near_n = scatter_near(npart, nrb1, 27)
    stat = jnp.concatenate([st0, st1, st2, jnp.zeros((5, nat), F32)], axis=0)
    st_snd[...] = stat

    for l in range(5):
        acc = jnp.zeros((ch, 128), F32)
        for k in range(l * l, (l + 1) * (l + 1)):
            acc = acc + lanes_dot(xn[k], dyb[k])
        gup[l] = acc
    gup[5] = lanes_dot(xn[0], da)
    ssend = []
    for j, dev in enumerate((t1, t2, t3)):
        c = remote(st_snd, st_all.at[j], 30 + j, {"tp": dev})
        c.start()
        ssend.append(c)
    near_n[0].wait_recv()
    nsb[...] = (npart[:, blk(t2), :].astype(F32) + nrb1[0].astype(F32)).astype(BF16)
    ex_up = remote(gup.at[:, theirs, :], gup_rb, 33, {"dp": odp})
    ex_up.start()
    far_n = remote(nsb, nrb2, 29, {"tp": t2})
    far_n.start()

    ex_dn.wait_recv()
    ddown_ref[:, mine, :] = (gdn[:, mine, :] + gdn_rb[...]).astype(BF16)
    near_d[1].wait_recv()
    far_d.wait_recv()
    own = dpart[:, blk(t), :].astype(F32) + rb1[1].astype(F32) + rb2[...].astype(F32)
    out_ref[...] = (xg[:, blk(t), :].astype(F32) + own).astype(BF16)
    bk_dn = remote(ddown_ref.at[:, mine, :], ddown_ref.at[:, mine, :], 34, {"dp": odp})
    bk_dn.start()

    ex_up.wait_recv()
    dup_ref[:, mine, :] = (gup[0:5, mine, :] + gup_rb[0:5]).astype(BF16)
    dgate_ref[mine, :] = (gup[5, mine, :] + gup_rb[5]).astype(BF16)
    for c in ssend:
        c.wait_recv()
    stat = st_snd[...] + st_all[0] + st_all[1] + st_all[2]
    bk_up = remote(dup_ref.at[:, mine, :], dup_ref.at[:, mine, :], 35, {"dp": odp})
    bk_up.start()
    bk_gt = remote(dgate_ref.at[mine, :], dgate_ref.at[mine, :], 36, {"dp": odp})
    bk_gt.start()
    b0 = stat[0:1] / ch
    b1 = stat[1:2] / ch
    b2 = (inv_v * inv_v * inv_v) * (stat[2:3] / (ch * (COEFS - 1)))
    near_n[1].wait_recv()
    far_n.wait_recv()
    for k in range(COEFS):
        dn = (npart[k, blk(t), :].astype(F32) + nrb1[1, k].astype(F32) + nrb2[k].astype(F32)).astype(BF16).astype(F32)
        dhat = dn * gcol[degree_of(k), blk(t), :]
        xk = xg[k, blk(t), :].astype(F32)
        if k == 0:
            dxk = inv_s * (dhat - b0 - (xk - mean_s) * inv_s * b1)
        else:
            dxk = inv_v * dhat - xk * b2
        dx_ref[k] = (dxk + gg[k, blk(t), :].astype(F32)).astype(BF16)

    bk_dn.wait_recv()
    bk_up.wait_recv()
    bk_gt.wait_recv()
    for c in far_g + fwd_x + fwd_g + gsend + near_d + near_n + ssend + [near_x, near_g, far_d, far_n, ex_dn, ex_up, bk_dn, bk_up, bk_gt]:
        c.wait_send()


def solution(mesh):
    tp_size = mesh.shape['tp']
    act_spec = P('dp', None, 'tp')
    in_specs = (act_spec, P(None, 'tp'), P(None, None, 'tp'), P(None, 'tp'), P(None, 'tp', None), P(None, None), P(None, None), act_spec)
    out_specs = (act_spec, act_spec, P(None, None, 'tp'), P(None, 'tp'), P(None, 'tp', None))

    def local_step(x_loc, gain_loc, up_loc, gate_loc, down_loc, to_grid, from_grid, grad_loc):
        nat, coefs, cl = x_loc.shape
        ch = cl * tp_size
        grid_pts = to_grid.shape[1]
        pp = -(-grid_pts // 16) * 16
        xt = x_loc.transpose(1, 2, 0)
        gt = grad_loc.transpose(1, 2, 0)
        any_spec = pl.BlockSpec(memory_space=pl.ANY)
        vmem = pl.BlockSpec(memory_space=pltpu.VMEM)
        full = pltpu.VMEM((coefs, ch, nat), BF16)
        blkb = pltpu.VMEM((coefs, cl, nat), BF16)
        sq = lambda n, d: pltpu.VMEM((n, 128, 128), d)
        outs = pl.pallas_call(
            functools.partial(kernel, tp_size, grid_pts),
            out_shape=(jax.ShapeDtypeStruct(xt.shape, BF16), jax.ShapeDtypeStruct(xt.shape, BF16),
                       jax.ShapeDtypeStruct(up_loc.shape, BF16), jax.ShapeDtypeStruct(gate_loc.shape, BF16),
                       jax.ShapeDtypeStruct(down_loc.shape, BF16)),
            in_specs=[any_spec] * 8,
            out_specs=[vmem] * 5,
            scratch_shapes=[
                full, full, full, full, full, full, full,
                pltpu.VMEM((64 * YSTRIDE, 128), F32), pltpu.VMEM((64 * YSTRIDE, 128), F32),
                pltpu.VMEM((KPAD * 136, 128), F32), pltpu.VMEM((64 * pp, 256), BF16),
                pltpu.VMEM(gain_loc.shape, F32), pltpu.VMEM((8, 128), F32), pltpu.VMEM((3, 8, 128), F32), sq(5, F32),
                sq(5, BF16), pltpu.VMEM((128, 128), BF16), sq(5, BF16), sq(5, BF16), pltpu.VMEM((128, 128), BF16), sq(5, BF16),
                pltpu.VMEM(to_grid.shape, F32), pltpu.VMEM(from_grid.shape[::-1], F32),
                pltpu.VMEM((pp, KPAD), BF16), pltpu.VMEM((KPAD, 384), BF16), pltpu.VMEM((pp, KPAD), BF16), pltpu.VMEM((KPAD, 384), BF16),
                pltpu.VMEM((2, coefs, cl, nat), BF16), blkb, blkb, pltpu.VMEM((2, coefs, cl, nat), BF16), blkb, blkb,
                pltpu.VMEM((8, 128), F32), pltpu.VMEM((3, 8, 128), F32),
                sq(5, F32), pltpu.VMEM((5, 64, 128), F32), sq(6, F32), pltpu.VMEM((6, 64, 128), F32),
                pltpu.VMEM((128, nat), BF16),
                pltpu.SemaphoreType.DMA((8,)), pltpu.SemaphoreType.DMA((40,)), pltpu.SemaphoreType.DMA((40,)),
            ],
            compiler_params=pltpu.CompilerParams(collective_id=0, has_side_effects=True, vmem_limit_bytes=60 * 1024 * 1024),
        )(xt, gain_loc, up_loc, gate_loc, down_loc, to_grid, from_grid.T, gt)
        out_t, dx_t, d_up, d_gate, d_down = outs
        return out_t.transpose(2, 0, 1), dx_t.transpose(2, 0, 1), d_up, d_gate, d_down

    return jax.shard_map(local_step, mesh=mesh, in_specs=in_specs, out_specs=out_specs, check_vma=False)
```

time: 130 us -> 70.2 us (0.54)
  Pallas kernels: 0 us -> 64.6 us
  blocking collectives: 56.4 us -> 0 us
  matrix products: 40.8 us -> 0 us
  between operations: 14.5 us -> 0.66 us
  other arithmetic: 7.97 us -> 0 us
  local copies, waits for them, and re-layouts: 9.89 us -> 4.7 us
    pallas_call x0 -> x1, Pallas kernels: none -> 64.6 us  [local_step(): pl.pallas_call(functools.partial(kernel, tp_size, grid_pts), out_shape=(j...]
    dot_general x12 -> x0, matrix products: 40.8 us -> none  [the longest x1 15.8 us: hidden_block(): jnp.einsum('ngh,kg->nkh', d_pre_grid, grid_in, preferred_element_type=jnp...]
    psum x3 -> x0, blocking collectives: 33.8 us -> none  [the longest x1 19.4 us: local_step(): d_up = lax.psum(g_up, 'dp').astype(jnp.bfloat16)]
    all_gather x2 -> x0, blocking collectives: 22.6 us -> none  [the longest x1 11.7 us: local_step(): xn_full = lax.all_gather(xn_loc, 'tp', axis=2, tiled=True)]
    convert_element_type x4 -> x0, other arithmetic: 4.33 us -> none  [the longest x1 1.67 us: local_step(): out_loc = (x_f + ffn_delta.astype(jnp.float32)).astype(jnp.bfloat16)]
    unnamed x34 -> x13, local copies, waits for them, and re-layouts: 1.34 us -> 4.7 us
    concatenate x4 -> x0, other arithmetic: 2.45 us -> none  [the longest x1 1.46 us: hidden_block(): mixed_act = jnp.concatenate([gate_val[:, None, :], back_proj], axis=1)]
    concatenate x3 -> x0, local copies, waits for them, and re-layouts: 2.33 us -> none  [the longest x1 2.17 us: hidden_block(): mixed_act = jnp.concatenate([gate_val[:, None, :], back_proj], axis=1)]
  transfers between devices with their start and end apart: 2 -> 0, of which waited for: 0 -> 0; matrix products, arithmetic and copies ran while one was open for 16% -> 0% of each run, Pallas kernels for 0% -> 0%
where the time goes in v1:
time: 70.2 us; the launch traced here: 70 us
  Pallas kernels  64.6 us (92%)
  local copies, waits for them, and re-layouts  4.7 us (7%)
    pallas_call x1, Pallas kernels, local_step(): pl.pallas_call(functools.partial(kernel, tp_size, grid_pts), out_shape=(j...  64.6 us
    unnamed x13, local copies, waits for them, and re-layouts  4.7 us

profile of v1, /device:TPU:0, one launch (start us, length us, event | category | flops | bytes accessed | tf_op | source)
XLA Modules:
  0.0 70.0 jit_solution(16558317859226013511)
XLA Ops:
  0.6 64.6 %shard_map.119 = (bf16[25,32,128]{2,1,0:T(8,128)(2,1)}, bf16[25,32,128]{2,1,0:T(8,128)(2,1)}, bf16[5,128,128]{2,1,0:T(8,128)(2,1)}, bf16[128,128]{1,0:T(8,128)(2,1)}, bf16[5,128,128]{2,1,0:T(8,128)(2,1)}) custom-call(bf16[25,32,128]{2,1,0:T(8,128)(2,1)} %bitcast.7, f32[5,32]{1,0:T(8,128)} %gain_hbm.1, bf16[5,128,128]{2,1,0:T(8,128)(2,1)} %up_hbm.1, ...), custom_call_target="tpu_custom_call" | custom-call | tf_op jit(solution)/shard_map/pallas_call | solution.py:345
  65.3 0.0 copy-start
  65.3 1.7 %copy.18 = bf16[128,25,32]{0,2,1:T(8,128)(2,1)} copy(bf16[128,25,32]{0,2,1:T(8,128)(2,1)} %bitcast.6) | data formatting | bytes 409600
  67.0 0.0 copy-done
  67.0 0.0 copy-start.2
  67.0 0.7 copy.19
  67.6 0.3 copy-done.2
  68.0 0.0 copy-start.3
  68.0 0.0 copy-start.1
  68.0 0.7 copy.20
  68.6 0.1 copy-done.3
  68.7 0.6 copy.21
  69.3 0.0 copy-done.1
  69.3 0.7 copy.22
Async XLA Ops:
  65.3 1.7 %copy-start = (bf16[25,32,128]{2,1,0:T(8,128)(2,1)S(1)}, bf16[25,32,128]{2,1,0:T(8,128)(2,1)}, u32[]{:S(2)}) copy-start(bf16[25,32,128]{2,1,0:T(8,128)(2,1)} %get-tuple-element.11) | copy-start | bytes 614404
  67.0 1.0 %copy-start.2 = (bf16[5,128,128]{2,1,0:T(8,128)(2,1)S(1)}, bf16[5,128,128]{2,1,0:T(8,128)(2,1)}, u32[]{:S(2)}) copy-start(bf16[5,128,128]{2,1,0:T(8,128)(2,1)} %get-tuple-element.22) | copy-start | bytes 491524
  68.0 0.8 %copy-start.3 = (bf16[128,128]{1,0:T(8,128)(2,1)S(1)}, bf16[128,128]{1,0:T(8,128)(2,1)}, u32[]{:S(2)}) copy-start(bf16[128,128]{1,0:T(8,128)(2,1)} %get-tuple-element.23) | copy-start | bytes 98308
  68.0 1.4 %copy-start.1 = (bf16[5,128,128]{2,1,0:T(8,128)(2,1)S(1)}, bf16[5,128,128]{2,1,0:T(8,128)(2,1)}, u32[]{:S(2)}) copy-start(bf16[5,128,128]{2,1,0:T(8,128)(2,1)} %get-tuple-element.24) | copy-start | bytes 491524

commit v2 on v1

--- a/solution.py
+++ b/solution.py
@@ -34,8 +34,9 @@
            xg, gg, xn, mb, dyb, dpart, npart, ya, yb, zs, hs,
            gain_in, gain_snd, gain_all, gcol, up, gate, down, upt, gatet, downt,
            tog, frg, tt, tmat, fmat, ft, rb1, sb, rb2, nrb1, nsb, nrb2,
-           st_snd, st_all, gdn, gdn_rb, gup, gup_rb, amat,
+           st_snd, st_all, gdn, gdn_rb, gup, gup_rb, amat, sbuf0, sbuf1, gbuf0, gbuf1,
            loc_sem, snd_sem, rcv_sem):
+    sbuf, gbuf = (sbuf0, sbuf1), (gbuf0, gbuf1)
     dp = lax.axis_index("dp")
     t = lax.axis_index("tp")
     core = lax.rem(t, 2)
@@ -183,17 +184,30 @@
         zs[pl.ds(i, KPAD, stride=136), :] = r[:, 0:128]
         zs[pl.ds(i + 64, KPAD, stride=136), :] = r[:, 128:256]
 
+    def stage_u(p, dst):
+        dst[...] = rows_dot(tt[...], pair(p)).astype(BF16)
+
+    def stage_s(p, src, dst):
+        hb = src[...]
+        hs[pl.ds(pl.multiple_of(p * pp, 16), pp), :] = hb
+        h = hb.astype(F32)
+        dst[...] = (h * (1.0 + jnp.tanh(h))).astype(BF16)
+
+    def stage_z(p, src, lhs):
+        put(p, rows_dot(lhs[:, 0:pp], src[...]))
+
+    stage_u(0, gbuf[0])
+
     def fwd_body(it, carry):
         for j in range(UNROLL):
-            i = it * UNROLL + j
-            hb = rows_dot(tt[...], pair(i)).astype(BF16)
-            hs[pl.ds(pl.multiple_of(i * pp, 16), pp), :] = hb
-            h = hb.astype(F32)
-            s = (h * (1.0 + jnp.tanh(h))).astype(BF16)
-            put(i, rows_dot(ft[:, 0:pp], s))
+            p = it * UNROLL + j
+            stage_z(jnp.maximum(p - 1, 0), sbuf[(j + 1) % 2], ft)
+            stage_u(p + 1, gbuf[(j + 1) % 2])
+            stage_s(p, gbuf[j % 2], sbuf[j % 2])
         return carry
 
     lax.fori_loop(0, 64 // UNROLL, fwd_body, 0)
+    stage_z(63, sbuf[1], ft)
 
     for k in range(1, COEFS):
         mb[k] = zs[k * 136:k * 136 + 128, :].astype(BF16)
@@ -233,17 +247,27 @@
     ex_dn = remote(gdn.at[:, theirs, :], gdn_rb, 26, {"dp": odp})
     ex_dn.start()
 
+    def stage_g(p, dst):
+        dst[...] = rows_dot(fmat[...], pair(p)).astype(BF16)
+
+    def stage_e(p, src, dst):
+        dg = src[...].astype(F32)
+        h = hs[pl.ds(pl.multiple_of(p * pp, 16), pp), :].astype(F32)
+        w = 1.0 + jnp.tanh(h)
+        dst[...] = (dg * (w * (1.0 + h * (2.0 - w)))).astype(BF16)
+
+    stage_g(0, gbuf[0])
+
     def bwd_body(it, carry):
         for j in range(UNROLL):
-            i = it * UNROLL + j
-            dg = rows_dot(fmat[...], pair(i)).astype(BF16).astype(F32)
-            h = hs[pl.ds(pl.multiple_of(i * pp, 16), pp), :].astype(F32)
-            w = 1.0 + jnp.tanh(h)
-            dpre = (dg * (w * (1.0 + h * (2.0 - w)))).astype(BF16)
-            put(i, rows_dot(tmat[:, 0:pp], dpre))
+            p = it * UNROLL + j
+            stage_z(jnp.maximum(p - 1, 0), sbuf[(j + 1) % 2], tmat)
+            stage_g(p + 1, gbuf[(j + 1) % 2])
+            stage_e(p, gbuf[j % 2], sbuf[j % 2])
         return carry
 
     lax.fori_loop(0, 64 // UNROLL, bwd_body, 0)
+    stage_z(63, sbuf[1], tmat)
 
     for k in range(COEFS):
         dyb[k] = zs[k * 136:k * 136 + 128, :].astype(BF16)
@@ -351,8 +375,8 @@
             out_specs=[vmem] * 5,
             scratch_shapes=[
                 full, full, full, full, full, full, full,
-                pltpu.VMEM((64 * YSTRIDE, 128), F32), pltpu.VMEM((64 * YSTRIDE, 128), F32),
-                pltpu.VMEM((KPAD * 136, 128), F32), pltpu.VMEM((64 * pp, 256), BF16),
+                pltpu.VMEM((65 * YSTRIDE, 128), F32), pltpu.VMEM((65 * YSTRIDE, 128), F32),
+                pltpu.VMEM((KPAD * 136, 128), F32), pltpu.VMEM((65 * pp, 256), BF16),
                 pltpu.VMEM(gain_loc.shape, F32), pltpu.VMEM((8, 128), F32), pltpu.VMEM((3, 8, 128), F32), sq(5, F32),
                 sq(5, BF16), pltpu.VMEM((128, 128), BF16), sq(5, BF16), sq(5, BF16), pltpu.VMEM((128, 128), BF16), sq(5, BF16),
                 pltpu.VMEM(to_grid.shape, F32), pltpu.VMEM(from_grid.shape[::-1], F32),
@@ -361,6 +385,7 @@
                 pltpu.VMEM((8, 128), F32), pltpu.VMEM((3, 8, 128), F32),
                 sq(5, F32), pltpu.VMEM((5, 64, 128), F32), sq(6, F32), pltpu.VMEM((6, 64, 128), F32),
                 pltpu.VMEM((128, nat), BF16),
+                pltpu.VMEM((pp, 256), BF16), pltpu.VMEM((pp, 256), BF16), pltpu.VMEM((pp, 256), BF16), pltpu.VMEM((pp, 256), BF16),
                 pltpu.SemaphoreType.DMA((8,)), pltpu.SemaphoreType.DMA((40,)), pltpu.SemaphoreType.DMA((40,)),
             ],
             compiler_params=pltpu.CompilerParams(collective_id=0, has_side_effects=True, vmem_limit_bytes=60 * 1024 * 1024),

time: 70.2 us -> 52.4 us (0.75)
  Pallas kernels: 64.6 us -> 46.9 us
    pallas_call x1, Pallas kernels: 64.6 us -> 46.9 us  [local_step(): pl.pallas_call(functools.partial(kernel, tp_size, grid_pts), out_shape=(j...]
where the time goes in v2:
time: 52.4 us; the launch traced here: 52.2 us
  Pallas kernels  46.9 us (90%)
  local copies, waits for them, and re-layouts  4.7 us (9%)
  between operations  0.66 us (1%)
    pallas_call x1, Pallas kernels, local_step(): pl.pallas_call(functools.partial(kernel, tp_size, grid_pts), out_shape=(j...  46.9 us
    unnamed x13, local copies, waits for them, and re-layouts  4.7 us

profile of v2, /device:TPU:0, one launch (start us, length us, event | category | flops | bytes accessed | tf_op | source)
XLA Modules:
  0.0 52.2 jit_solution(12957284660357667797)
XLA Ops:
  0.6 46.9 %shard_map.119 = (bf16[25,32,128]{2,1,0:T(8,128)(2,1)}, bf16[25,32,128]{2,1,0:T(8,128)(2,1)}, bf16[5,128,128]{2,1,0:T(8,128)(2,1)}, bf16[128,128]{1,0:T(8,128)(2,1)}, bf16[5,128,128]{2,1,0:T(8,128)(2,1)}) custom-call(bf16[25,32,128]{2,1,0:T(8,128)(2,1)} %bitcast.7, f32[5,32]{1,0:T(8,128)} %gain_hbm.1, bf16[5,128,128]{2,1,0:T(8,128)(2,1)} %up_hbm.1, ...), custom_call_target="tpu_custom_call" | custom-call | tf_op jit(solution)/shard_map/pallas_call | solution.py:369
  47.5 0.0 copy-start
  47.5 1.7 %copy.18 = bf16[128,25,32]{0,2,1:T(8,128)(2,1)} copy(bf16[128,25,32]{0,2,1:T(8,128)(2,1)} %bitcast.6) | data formatting | bytes 409600
  49.2 0.0 copy-done
  49.2 0.0 copy-start.2
  49.2 0.7 %copy.19 = bf16[128,25,32]{0,2,1:T(8,128)(2,1)} copy(bf16[128,25,32]{0,2,1:T(8,128)(2,1)S(1)} %bitcast.5) | data formatting | bytes 409600
  49.9 0.3 copy-done.2
  50.2 0.0 copy-start.3
  50.2 0.0 copy-start.1
  50.2 0.7 %copy.20 = bf16[5,128,128]{2,1,0:T(8,128)(2,1)} copy(bf16[5,128,128]{2,1,0:T(8,128)(2,1)S(1)} %copy-done.2) | data formatting | bytes 327680
  50.8 0.1 copy-done.3
  50.9 0.6 %copy.21 = bf16[128,128]{1,0:T(8,128)(2,1)} copy(bf16[128,128]{1,0:T(8,128)(2,1)S(1)} %copy-done.3) | data formatting | bytes 65536
  51.5 0.0 copy-done.1
  51.5 0.7 %copy.22 = bf16[5,128,128]{2,1,0:T(8,128)(2,1)} copy(bf16[5,128,128]{2,1,0:T(8,128)(2,1)S(1)} %copy-done.1) | data formatting | bytes 327680
Async XLA Ops:
  47.5 1.7 %copy-start = (bf16[25,32,128]{2,1,0:T(8,128)(2,1)S(1)}, bf16[25,32,128]{2,1,0:T(8,128)(2,1)}, u32[]{:S(2)}) copy-start(bf16[25,32,128]{2,1,0:T(8,128)(2,1)} %get-tuple-element.11) | copy-start | bytes 614404
  49.2 1.0 %copy-start.2 = (bf16[5,128,128]{2,1,0:T(8,128)(2,1)S(1)}, bf16[5,128,128]{2,1,0:T(8,128)(2,1)}, u32[]{:S(2)}) copy-start(bf16[5,128,128]{2,1,0:T(8,128)(2,1)} %get-tuple-element.22) | copy-start | bytes 491524
  50.2 0.8 %copy-start.3 = (bf16[128,128]{1,0:T(8,128)(2,1)S(1)}, bf16[128,128]{1,0:T(8,128)(2,1)}, u32[]{:S(2)}) copy-start(bf16[128,128]{1,0:T(8,128)(2,1)} %get-tuple-element.23) | copy-start | bytes 98308
  50.2 1.4 %copy-start.1 = (bf16[5,128,128]{2,1,0:T(8,128)(2,1)S(1)}, bf16[5,128,128]{2,1,0:T(8,128)(2,1)}, u32[]{:S(2)}) copy-start(bf16[5,128,128]{2,1,0:T(8,128)(2,1)} %get-tuple-element.24) | copy-start | bytes 491524

commit v3 on v2

--- a/solution.py
+++ b/solution.py
@@ -15,6 +15,7 @@
 KPAD = 32
 YSTRIDE = 40
 UNROLL = 2
+QR = 32
 
 
 def degree_of(k):
@@ -34,7 +35,7 @@
            xg, gg, xn, mb, dyb, dpart, npart, ya, yb, zs, hs,
            gain_in, gain_snd, gain_all, gcol, up, gate, down, upt, gatet, downt,
            tog, frg, tt, tmat, fmat, ft, rb1, sb, rb2, nrb1, nsb, nrb2,
-           st_snd, st_all, gdn, gdn_rb, gup, gup_rb, amat, sbuf0, sbuf1, gbuf0, gbuf1,
+           st_snd, st_all, gdn, gdn_rb, gup, gup_rb, gfin, gfin_dn, amat, sbuf0, sbuf1, gbuf0, gbuf1,
            loc_sem, snd_sem, rcv_sem):
     sbuf, gbuf = (sbuf0, sbuf1), (gbuf0, gbuf1)
     dp = lax.axis_index("dp")
@@ -61,29 +62,30 @@
         return pltpu.make_async_remote_copy(src_ref=src, dst_ref=dst, send_sem=snd_sem.at[i], recv_sem=rcv_sem.at[i],
                                             device_id=dev, device_id_type=MESH)
 
+    ksplit = ((0, 7), (7, 13), (13, 19), (19, 25))
+    c_x = [local(x_hbm.at[k0:k1], xg.at[k0:k1, blk(t), :], 7 + j) for j, (k0, k1) in enumerate(ksplit)]
     c_gain = local(gain_hbm, gain_in, 0)
-    c_x = local(x_hbm, xg.at[:, blk(t), :], 1)
     c_tog = local(tog_hbm, tog, 2)
     c_frg = local(frg_hbm, frg, 3)
     c_up = local(up_hbm, up, 4)
     c_gate = local(gate_hbm, gate, 5)
     c_down = local(down_hbm, down, 6)
-    c_g = local(g_hbm, gg.at[:, blk(t), :], 7)
+    c_g = local(g_hbm, gg.at[:, blk(t), :], 1)
 
     barrier = pltpu.get_barrier_semaphore()
     for dev in ({"tp": t1}, {"tp": t2}, {"tp": t3}, {"dp": odp}):
         pl.semaphore_signal(barrier, inc=1, device_id=dev, device_id_type=MESH)
     pl.semaphore_wait(barrier, 4)
 
-    ksplit = ((0, 7), (7, 13), (13, 19), (19, 25))
-
-    def gather_start(src, dst, base):
-        far, near = [], None
+    def gather_start(dst, base, ready=None):
+        far = []
         for j, (k0, k1) in enumerate(ksplit):
-            c = remote(src.at[k0:k1], dst.at[k0:k1, blk(t), :], base + j, {"tp": t2})
+            if ready:
+                ready[j].wait()
+            c = remote(dst.at[k0:k1, blk(t), :], dst.at[k0:k1, blk(t), :], base + j, {"tp": t2})
             c.start()
             far.append(c)
-        near = remote(src, dst.at[:, blk(t), :], base + 4, {"tp": t1})
+        near = remote(dst.at[:, blk(t), :], dst.at[:, blk(t), :], base + 4, {"tp": t1})
         near.start()
         return far, near
 
@@ -99,7 +101,7 @@
             c.wait_recv()
         return fwd
 
-    far_x, near_x = gather_start(x_hbm, xg, 0)
+    far_x, near_x = gather_start(xg, 0, c_x)
 
     gain_snd[...] = jnp.zeros_like(gain_snd)
     c_gain.wait()
@@ -141,11 +143,11 @@
     for l in range(5):
         gcol[l] = jnp.broadcast_to(gain_full[l:l + 1, :], (ch, ch)).T
 
-    c_x.wait()
     fwd_x = gather_finish(far_x, near_x, xg, 0)
     for c in far_x:
         c.wait_send()
-    far_g, near_g = gather_start(g_hbm, gg, 10)
+    c_g.wait()
+    far_g, near_g = gather_start(gg, 10)
 
     x0 = xg[0].astype(F32)
     mean_s = jnp.sum(x0, axis=0, keepdims=True) / ch
@@ -225,7 +227,6 @@
     near_d = scatter_near(dpart, rb1, 23)
 
     fwd_g = gather_finish(far_g, near_g, gg, 10)
-    c_g.wait()
     spread(lambda k: gg[k], lambda l: down[l])
     dm0 = rows_dot(down[0], gg[0]).astype(BF16).astype(F32)
     a_h = amat[...].astype(F32) * 0.5
@@ -239,6 +240,7 @@
         for k in range(l * l, (l + 1) * (l + 1)):
             acc = acc + lanes_dot(mb[k], gg[k])
         gdn[l] = acc
+    gdn[5] = lanes_dot(da, xn[0])
     far_d = remote(sb, rb2, 25, {"tp": t2})
     far_d.start()
     half = 64
@@ -266,86 +268,138 @@
             stage_e(p, gbuf[j % 2], sbuf[j % 2])
         return carry
 
-    lax.fori_loop(0, 64 // UNROLL, bwd_body, 0)
+    def grad_up(k_rows, lo):
+        for l in range(5):
+            acc = jnp.zeros((2 * QR, ch), F32)
+            for k in range(l * l, (l + 1) * (l + 1)):
+                dy = jnp.concatenate([zs[k * 136 + lo:k * 136 + lo + QR, :].astype(BF16),
+                                      zs[k * 136 + 64 + lo:k * 136 + 64 + lo + QR, :].astype(BF16)], axis=0)
+                dyb[k, lo:lo + QR, :] = dy[0:QR]
+                dyb[k, 64 + lo:64 + lo + QR, :] = dy[QR:2 * QR]
+                acc = acc + lanes_dot(dy, xn[k])
+            gup[l, lo:lo + QR, :] = acc[0:QR]
+            gup[l, 64 + lo:64 + lo + QR, :] = acc[QR:2 * QR]
+
+    def rows_of(d, lo):
+        return pl.ds(pl.multiple_of(d * half + lo, QR), QR)
+
+    mid_steps = (QR + 2) // UNROLL
+    lax.fori_loop(0, mid_steps, bwd_body, 0)
+
+    grad_up(None, 0)
+    ex_up0 = remote(gup.at[:, rows_of(odp, 0), :], gup_rb.at[:, 0:QR, :], 33, {"dp": odp})
+    ex_up0.start()
+    ex_dn.wait_recv()
+    gfin_dn[:, mine, :] = (gdn[:, mine, :] + gdn_rb[...]).astype(BF16)
+    near_d[1].wait_recv()
+    far_d.wait_recv()
+    own = dpart[:, blk(t), :].astype(F32) + rb1[1].astype(F32) + rb2[...].astype(F32)
+    out_ref[...] = (xg[:, blk(t), :].astype(F32) + own).astype(BF16)
+    bk_dn = remote(gfin_dn.at[:, mine, :], gfin_dn.at[:, mine, :], 34, {"dp": odp})
+    bk_dn.start()
+
+    lax.fori_loop(mid_steps, 64 // UNROLL, bwd_body, 0)
     stage_z(63, sbuf[1], tmat)
 
     for k in range(COEFS):
-        dyb[k] = zs[k * 136:k * 136 + 128, :].astype(BF16)
+        for o in (QR, 64 + QR):
+            dyb[k, o:o + QR, :] = zs[k * 136 + o:k * 136 + o + QR, :].astype(BF16)
+    nsplit = ((0, 9), (9, 16), (16, 25))
+    near_n = []
     s3 = jnp.zeros((ch, nat), F32)
+    for j, (k0, k1) in enumerate(nsplit):
+        for k in range(k0, k1):
+            r = rows_dot(up[degree_of(k)], dyb[k])
+            if k == 0:
+                r = r + rows_dot(gate[...], da)
+            npart[k] = r.astype(BF16)
+        c = remote(npart.at[k0:k1, blk(t3), :], nrb1.at[0, k0:k1], 27 + j, {"tp": t1})
+        c.start()
+        near_n.append(c)
+    near_o = remote(npart.at[:, blk(t1), :], nrb1.at[1], 30, {"tp": t1})
+    near_o.start()
+    ex_up0.wait_recv()
+    gfin[:, rows_of(dp, 0), :] = (gup[:, rows_of(dp, 0), :] + gup_rb[:, 0:QR, :]).astype(BF16)
     for k in range(COEFS):
-        r = rows_dot(up[degree_of(k)], dyb[k])
-        if k == 0:
-            r = r + rows_dot(gate[...], da)
-        rb = r.astype(BF16)
-        npart[k] = rb
-        rf = rb.astype(F32) * gcol[degree_of(k)]
+        rf = npart[k].astype(F32) * gcol[degree_of(k)]
         if k == 0:
             st0 = jnp.sum(rf, axis=0, keepdims=True)
             st1 = jnp.sum(rf * hat_s, axis=0, keepdims=True)
         else:
             s3 = s3 + rf * xg[k].astype(F32)
     st2 = jnp.sum(s3, axis=0, keepdims=True)
-    near_n = scatter_near(npart, nrb1, 27)
-    stat = jnp.concatenate([st0, st1, st2, jnp.zeros((5, nat), F32)], axis=0)
-    st_snd[...] = stat
-
-    for l in range(5):
-        acc = jnp.zeros((ch, 128), F32)
-        for k in range(l * l, (l + 1) * (l + 1)):
-            acc = acc + lanes_dot(xn[k], dyb[k])
-        gup[l] = acc
-    gup[5] = lanes_dot(xn[0], da)
+    st_snd[...] = jnp.concatenate([st0, st1, st2, jnp.zeros((5, nat), F32)], axis=0)
+    bk_up0 = remote(gfin.at[:, rows_of(dp, 0), :], gfin.at[:, rows_of(dp, 0), :], 35, {"dp": odp})
+    bk_up0.start()
+
+    far_n = []
+
+    def far_step(j):
+        k0, k1 = nsplit[j]
+        near_n[j].wait_recv()
+        nsb[k0:k1] = (npart[k0:k1, blk(t2), :].astype(F32) + nrb1[0, k0:k1].astype(F32)).astype(BF16)
+
+    def far_send(j):
+        k0, k1 = nsplit[j]
+        c = remote(nsb.at[k0:k1], nrb2.at[k0:k1], 41 + j, {"tp": t2})
+        c.start()
+        far_n.append(c)
+
+    far_step(0)
+    grad_up(None, QR)
+    far_send(0)
+    ex_up1 = remote(gup.at[:, rows_of(odp, QR), :], gup_rb.at[:, QR:2 * QR, :], 36, {"dp": odp})
+    ex_up1.start()
+    far_step(1)
+    far_step(2)
+    far_send(1)
+    far_send(2)
     ssend = []
     for j, dev in enumerate((t1, t2, t3)):
-        c = remote(st_snd, st_all.at[j], 30 + j, {"tp": dev})
+        c = remote(st_snd, st_all.at[j], 37 + j, {"tp": dev})
         c.start()
         ssend.append(c)
-    near_n[0].wait_recv()
-    nsb[...] = (npart[:, blk(t2), :].astype(F32) + nrb1[0].astype(F32)).astype(BF16)
-    ex_up = remote(gup.at[:, theirs, :], gup_rb, 33, {"dp": odp})
-    ex_up.start()
-    far_n = remote(nsb, nrb2, 29, {"tp": t2})
-    far_n.start()
-
-    ex_dn.wait_recv()
-    ddown_ref[:, mine, :] = (gdn[:, mine, :] + gdn_rb[...]).astype(BF16)
-    near_d[1].wait_recv()
-    far_d.wait_recv()
-    own = dpart[:, blk(t), :].astype(F32) + rb1[1].astype(F32) + rb2[...].astype(F32)
-    out_ref[...] = (xg[:, blk(t), :].astype(F32) + own).astype(BF16)
-    bk_dn = remote(ddown_ref.at[:, mine, :], ddown_ref.at[:, mine, :], 34, {"dp": odp})
-    bk_dn.start()
-
-    ex_up.wait_recv()
-    dup_ref[:, mine, :] = (gup[0:5, mine, :] + gup_rb[0:5]).astype(BF16)
-    dgate_ref[mine, :] = (gup[5, mine, :] + gup_rb[5]).astype(BF16)
+
+    bk_dn.wait_recv()
+    ddown_ref[...] = gfin_dn[0:5]
+    dgate_ref[...] = gfin_dn[5].astype(F32).T.astype(BF16)
+    ex_up1.wait_recv()
+    gfin[:, rows_of(dp, QR), :] = (gup[:, rows_of(dp, QR), :] + gup_rb[:, QR:2 * QR, :]).astype(BF16)
     for c in ssend:
         c.wait_recv()
     stat = st_snd[...] + st_all[0] + st_all[1] + st_all[2]
-    bk_up = remote(dup_ref.at[:, mine, :], dup_ref.at[:, mine, :], 35, {"dp": odp})
-    bk_up.start()
-    bk_gt = remote(dgate_ref.at[mine, :], dgate_ref.at[mine, :], 36, {"dp": odp})
-    bk_gt.start()
     b0 = stat[0:1] / ch
     b1 = stat[1:2] / ch
     b2 = (inv_v * inv_v * inv_v) * (stat[2:3] / (ch * (COEFS - 1)))
-    near_n[1].wait_recv()
-    far_n.wait_recv()
-    for k in range(COEFS):
-        dn = (npart[k, blk(t), :].astype(F32) + nrb1[1, k].astype(F32) + nrb2[k].astype(F32)).astype(BF16).astype(F32)
-        dhat = dn * gcol[degree_of(k), blk(t), :]
-        xk = xg[k, blk(t), :].astype(F32)
-        if k == 0:
-            dxk = inv_s * (dhat - b0 - (xk - mean_s) * inv_s * b1)
-        else:
-            dxk = inv_v * dhat - xk * b2
-        dx_ref[k] = (dxk + gg[k, blk(t), :].astype(F32)).astype(BF16)
-
-    bk_dn.wait_recv()
-    bk_up.wait_recv()
-    bk_gt.wait_recv()
-    for c in far_g + fwd_x + fwd_g + gsend + near_d + near_n + ssend + [near_x, near_g, far_d, far_n, ex_dn, ex_up, bk_dn, bk_up, bk_gt]:
+    bk_up1 = remote(gfin.at[:, rows_of(dp, QR), :], gfin.at[:, rows_of(dp, QR), :], 40, {"dp": odp})
+    bk_up1.start()
+    near_o.wait_recv()
+    for j, (k0, k1) in enumerate(nsplit):
+        far_n[j].wait_recv()
+        for k in range(k0, k1):
+            dn = (npart[k, blk(t), :].astype(F32) + nrb1[1, k].astype(F32) + nrb2[k].astype(F32)).astype(BF16).astype(F32)
+            dhat = dn * gcol[degree_of(k), blk(t), :]
+            xk = xg[k, blk(t), :].astype(F32)
+            if k == 0:
+                dxk = inv_s * (dhat - b0 - (xk - mean_s) * inv_s * b1)
+            else:
+                dxk = inv_v * dhat - xk * b2
+            dx_ref[k] = (dxk + gg[k, blk(t), :].astype(F32)).astype(BF16)
+
+    bk_up0.wait_recv()
+    bk_up1.wait_recv()
+    for l in range(5):
+        dup_ref[l] = gfin[l].astype(F32).T.astype(BF16)
+    for c in far_g + fwd_x + fwd_g + gsend + near_d + near_n + far_n + ssend + [near_x, near_g, near_o, far_d, ex_dn, ex_up0, ex_up1, bk_dn, bk_up0, bk_up1]:
         c.wait_send()
+
+
+def flush(a, b, c, d, e, oa, ob, oc, od, oe, sem):
+    cs = [pltpu.make_async_copy(i, o, sem.at[j]) for j, (i, o) in enumerate(zip((a, b, c, d, e), (oa, ob, oc, od, oe)))]
+    for x in cs:
+        x.start()
+    for x in cs:
+        x.wait()
 
 
 def solution(mesh):
@@ -366,11 +420,10 @@
         full = pltpu.VMEM((coefs, ch, nat), BF16)
         blkb = pltpu.VMEM((coefs, cl, nat), BF16)
         sq = lambda n, d: pltpu.VMEM((n, 128, 128), d)
+        shapes = (xt.shape, xt.shape, up_loc.shape, gate_loc.shape, down_loc.shape)
         outs = pl.pallas_call(
             functools.partial(kernel, tp_size, grid_pts),
-            out_shape=(jax.ShapeDtypeStruct(xt.shape, BF16), jax.ShapeDtypeStruct(xt.shape, BF16),
-                       jax.ShapeDtypeStruct(up_loc.shape, BF16), jax.ShapeDtypeStruct(gate_loc.shape, BF16),
-                       jax.ShapeDtypeStruct(down_loc.shape, BF16)),
+            out_shape=tuple(pltpu.VMEM(sh, BF16) for sh in shapes),
             in_specs=[any_spec] * 8,
             out_specs=[vmem] * 5,
             scratch_shapes=[
@@ -383,14 +436,20 @@
                 pltpu.VMEM((pp, KPAD), BF16), pltpu.VMEM((KPAD, 384), BF16), pltpu.VMEM((pp, KPAD), BF16), pltpu.VMEM((KPAD, 384), BF16),
                 pltpu.VMEM((2, coefs, cl, nat), BF16), blkb, blkb, pltpu.VMEM((2, coefs, cl, nat), BF16), blkb, blkb,
                 pltpu.VMEM((8, 128), F32), pltpu.VMEM((3, 8, 128), F32),
-                sq(5, F32), pltpu.VMEM((5, 64, 128), F32), sq(6, F32), pltpu.VMEM((6, 64, 128), F32),
+                sq(6, F32), pltpu.VMEM((6, 64, 128), F32), sq(5, F32), pltpu.VMEM((5, 64, 128), F32), sq(5, BF16), sq(6, BF16),
                 pltpu.VMEM((128, nat), BF16),
                 pltpu.VMEM((pp, 256), BF16), pltpu.VMEM((pp, 256), BF16), pltpu.VMEM((pp, 256), BF16), pltpu.VMEM((pp, 256), BF16),
-                pltpu.SemaphoreType.DMA((8,)), pltpu.SemaphoreType.DMA((40,)), pltpu.SemaphoreType.DMA((40,)),
+                pltpu.SemaphoreType.DMA((12,)), pltpu.SemaphoreType.DMA((44,)), pltpu.SemaphoreType.DMA((44,)),
             ],
             compiler_params=pltpu.CompilerParams(collective_id=0, has_side_effects=True, vmem_limit_bytes=60 * 1024 * 1024),
         )(xt, gain_loc, up_loc, gate_loc, down_loc, to_grid, from_grid.T, gt)
-        out_t, dx_t, d_up, d_gate, d_down = outs
+        out_t, dx_t, d_up, d_gate, d_down = pl.pallas_call(
+            flush,
+            out_shape=tuple(jax.ShapeDtypeStruct(sh, BF16) for sh in shapes),
+            in_specs=[vmem] * 5,
+            out_specs=[any_spec] * 5,
+            scratch_shapes=[pltpu.SemaphoreType.DMA((5,))],
+        )(*[pltpu.with_memory_space_constraint(o, pltpu.VMEM) for o in outs])
         return out_t.transpose(2, 0, 1), dx_t.transpose(2, 0, 1), d_up, d_gate, d_down
 
     return jax.shard_map(local_step, mesh=mesh, in_specs=in_specs, out_specs=out_specs, check_vma=False)

time: 52.4 us -> 49.1 us (0.937)
  local copies, waits for them, and re-layouts: 4.7 us -> 0 us
  Pallas kernels: 46.9 us -> 48.4 us
    unnamed x13 -> x0, local copies, waits for them, and re-layouts: 4.7 us -> none
    pallas_call x1 -> x2, Pallas kernels: 46.9 us -> 48.4 us  [the longest x1 47.5 us: local_step(): pl.pallas_call(functools.partial(kernel, tp_size, grid_pts), out_shape=tu...]
where the time goes in v3:
time: 49.1 us; the launch traced here: 49 us
  Pallas kernels  48.4 us (99%)
  between operations  0.64 us (1%)
    pallas_call x1, Pallas kernels, local_step(): pl.pallas_call(functools.partial(kernel, tp_size, grid_pts), out_shape=tu...  47.5 us

profile of v3, /device:TPU:0, one launch (start us, length us, event | category | flops | bytes accessed | tf_op | source)
XLA Modules:
  0.0 49.0 jit_solution(18297730065088337760)
XLA Ops:
  0.6 47.5 %shard_map.119 = (bf16[25,32,128]{2,1,0:T(8,128)(2,1)S(1)}, bf16[25,32,128]{2,1,0:T(8,128)(2,1)S(1)}, bf16[5,128,128]{2,1,0:T(8,128)(2,1)S(1)}, bf16[128,128]{1,0:T(8,128)(2,1)S(1)}, bf16[5,128,128]{2,1,0:T(8,128)(2,1)S(1)}) custom-call(bf16[25,32,128]{2,1,0:T(8,128)(2,1)} %bitcast.5, f32[5,32]{1,0:T(8,128)} %gain_hbm.1, bf16[5,128,128]{2,1,0:T(8,128)(2,1)} %up_hbm.1, ...), custom_call_target="tpu_custom_call" | custom-call | tf_op jit(solution)/shard_map/pallas_call | solution.py:424
  48.1 0.9 %shard_map.120 = (bf16[25,32,128]{2,1,0:T(8,128)(2,1)}, bf16[25,32,128]{2,1,0:T(8,128)(2,1)}, bf16[5,128,128]{2,1,0:T(8,128)(2,1)}, bf16[128,128]{1,0:T(8,128)(2,1)}, bf16[5,128,128]{2,1,0:T(8,128)(2,1)}) custom-call(bf16[25,32,128]{2,1,0:T(8,128)(2,1)S(1)} %get-tuple-element.15.a, bf16[25,32,128]{2,1,0:T(8,128)(2,1)S(1)} %get-tuple-element.16.b, ...), custom_call_target="tpu_custom_call" | custom-call | tf_op jit(solution)/shard_map/pallas_call | solution.py:446

commit v4 on v3

--- a/solution.py
+++ b/solution.py
@@ -163,14 +163,25 @@
     for k in range(1, COEFS):
         xn[k] = (xg[k].astype(F32) * inv_v * gcol[degree_of(k)]).astype(BF16)
 
+    def by_degree(lhs_of, get, lo=0, hi=COEFS):
+        for l in range(5):
+            k = max(l * l, lo)
+            k1 = min((l + 1) * (l + 1), hi)
+            while k < k1:
+                n = min(2, k1 - k)
+                r = rows_dot(lhs_of(l), get(k) if n == 1 else jnp.concatenate([get(k), get(k + 1)], axis=1))
+                for j in range(n):
+                    yield k + j, r[:, nat * j:nat * (j + 1)]
+                k += n
+
+    def over_degree(a_of, b_of, l):
+        ks = range(l * l, (l + 1) * (l + 1))
+        return lanes_dot(jnp.concatenate([a_of(k) for k in ks], axis=1), jnp.concatenate([b_of(k) for k in ks], axis=1))
+
     def spread(get, lhs_of):
-        for l in range(5):
-            k0, k1 = l * l, (l + 1) * (l + 1)
-            lhs = lhs_of(l)
-            for k in range(k0, k1):
-                r = rows_dot(lhs, get(k))
-                ya[pl.ds(k, 64, stride=YSTRIDE), :] = r[0:64]
-                yb[pl.ds(k, 64, stride=YSTRIDE), :] = r[64:128]
+        for k, r in by_degree(lhs_of, get):
+            ya[pl.ds(k, 64, stride=YSTRIDE), :] = r[0:64]
+            yb[pl.ds(k, 64, stride=YSTRIDE), :] = r[64:128]
 
     spread(lambda k: xn[k], lambda l: upt[l])
     a_r = rows_dot(gatet[...], xn[0]).astype(BF16)
@@ -190,10 +201,11 @@
         dst[...] = rows_dot(tt[...], pair(p)).astype(BF16)
 
     def stage_s(p, src, dst):
-        hb = src[...]
-        hs[pl.ds(pl.multiple_of(p * pp, 16), pp), :] = hb
-        h = hb.astype(F32)
-        dst[...] = (h * (1.0 + jnp.tanh(h))).astype(BF16)
+        h = src[...].astype(F32)
+        w = 1.0 + jnp.tanh(h)
+        s = h * w
+        dst[...] = s.astype(BF16)
+        hs[pl.ds(pl.multiple_of(p * pp, 16), pp), :] = w + s * (2.0 - w)
 
     def stage_z(p, src, lhs):
         put(p, rows_dot(lhs[:, 0:pp], src[...]))
@@ -213,8 +225,8 @@
 
     for k in range(1, COEFS):
         mb[k] = zs[k * 136:k * 136 + 128, :].astype(BF16)
-    for k in range(COEFS):
-        dpart[k] = rows_dot(downt[degree_of(k)], mb[k]).astype(BF16)
+    for k, r in by_degree(lambda l: downt[l], lambda k: mb[k]):
+        dpart[k] = r.astype(BF16)
 
     def scatter_near(part, rb, base):
         cs = []
@@ -233,30 +245,25 @@
     w_a = 1.0 + jnp.tanh(a_h)
     da = (dm0 * (0.5 * w_a * (1.0 + a_h * (2.0 - w_a)))).astype(BF16)
 
+    for l in range(5):
+        gdn[l] = over_degree(lambda k: mb[k], lambda k: gg[k], l)
+    gdn[5] = lanes_dot(da, xn[0])
     near_d[0].wait_recv()
     sb[...] = (dpart[:, blk(t2), :].astype(F32) + rb1[0].astype(F32)).astype(BF16)
-    for l in range(5):
-        acc = jnp.zeros((128, ch), F32)
-        for k in range(l * l, (l + 1) * (l + 1)):
-            acc = acc + lanes_dot(mb[k], gg[k])
-        gdn[l] = acc
-    gdn[5] = lanes_dot(da, xn[0])
-    far_d = remote(sb, rb2, 25, {"tp": t2})
-    far_d.start()
     half = 64
     mine = pl.ds(pl.multiple_of(dp * half, half), half)
     theirs = pl.ds(pl.multiple_of(odp * half, half), half)
     ex_dn = remote(gdn.at[:, theirs, :], gdn_rb, 26, {"dp": odp})
     ex_dn.start()
+    far_d = remote(sb, rb2, 25, {"tp": t2})
+    far_d.start()
 
     def stage_g(p, dst):
         dst[...] = rows_dot(fmat[...], pair(p)).astype(BF16)
 
     def stage_e(p, src, dst):
-        dg = src[...].astype(F32)
-        h = hs[pl.ds(pl.multiple_of(p * pp, 16), pp), :].astype(F32)
-        w = 1.0 + jnp.tanh(h)
-        dst[...] = (dg * (w * (1.0 + h * (2.0 - w)))).astype(BF16)
+        gp = hs[pl.ds(pl.multiple_of(p * pp, 16), pp), :]
+        dst[...] = (src[...].astype(F32) * gp).astype(BF16)
 
     stage_g(0, gbuf[0])
 
@@ -268,15 +275,15 @@
             stage_e(p, gbuf[j % 2], sbuf[j % 2])
         return carry
 
-    def grad_up(k_rows, lo):
+    def grad_up(lo):
+        def dy(k):
+            return jnp.concatenate([dyb[k, lo:lo + QR, :], dyb[k, 64 + lo:64 + lo + QR, :]], axis=0)
+
+        for k in range(COEFS):
+            for o in (lo, 64 + lo):
+                dyb[k, o:o + QR, :] = zs[k * 136 + o:k * 136 + o + QR, :].astype(BF16)
         for l in range(5):
-            acc = jnp.zeros((2 * QR, ch), F32)
-            for k in range(l * l, (l + 1) * (l + 1)):
-                dy = jnp.concatenate([zs[k * 136 + lo:k * 136 + lo + QR, :].astype(BF16),
-                                      zs[k * 136 + 64 + lo:k * 136 + 64 + lo + QR, :].astype(BF16)], axis=0)
-                dyb[k, lo:lo + QR, :] = dy[0:QR]
-                dyb[k, 64 + lo:64 + lo + QR, :] = dy[QR:2 * QR]
-                acc = acc + lanes_dot(dy, xn[k])
+            acc = over_degree(dy, lambda k: xn[k], l)
             gup[l, lo:lo + QR, :] = acc[0:QR]
             gup[l, 64 + lo:64 + lo + QR, :] = acc[QR:2 * QR]
 
@@ -284,11 +291,15 @@
         return pl.ds(pl.multiple_of(d * half + lo, QR), QR)
 
     mid_steps = (QR + 2) // UNROLL
+    late_steps = 52 // UNROLL
     lax.fori_loop(0, mid_steps, bwd_body, 0)
 
-    grad_up(None, 0)
+    grad_up(0)
     ex_up0 = remote(gup.at[:, rows_of(odp, 0), :], gup_rb.at[:, 0:QR, :], 33, {"dp": odp})
     ex_up0.start()
+
+    lax.fori_loop(mid_steps, late_steps, bwd_body, 0)
+
     ex_dn.wait_recv()
     gfin_dn[:, mine, :] = (gdn[:, mine, :] + gdn_rb[...]).astype(BF16)
     near_d[1].wait_recv()
@@ -298,28 +309,52 @@
     bk_dn = remote(gfin_dn.at[:, mine, :], gfin_dn.at[:, mine, :], 34, {"dp": odp})
     bk_dn.start()
 
-    lax.fori_loop(mid_steps, 64 // UNROLL, bwd_body, 0)
+    lax.fori_loop(late_steps, 64 // UNROLL, bwd_body, 0)
     stage_z(63, sbuf[1], tmat)
 
-    for k in range(COEFS):
-        for o in (QR, 64 + QR):
-            dyb[k, o:o + QR, :] = zs[k * 136 + o:k * 136 + o + QR, :].astype(BF16)
+    def full_dy(k):
+        return jnp.concatenate([dyb[k, 0:QR, :], zs[k * 136 + QR:k * 136 + 64, :].astype(BF16),
+                                dyb[k, 64:64 + QR, :], zs[k * 136 + 64 + QR:k * 136 + 128, :].astype(BF16)], axis=0)
+
     nsplit = ((0, 9), (9, 16), (16, 25))
     near_n = []
-    s3 = jnp.zeros((ch, nat), F32)
     for j, (k0, k1) in enumerate(nsplit):
-        for k in range(k0, k1):
-            r = rows_dot(up[degree_of(k)], dyb[k])
+        for k, r in by_degree(lambda l: up[l], full_dy, k0, k1):
             if k == 0:
                 r = r + rows_dot(gate[...], da)
             npart[k] = r.astype(BF16)
         c = remote(npart.at[k0:k1, blk(t3), :], nrb1.at[0, k0:k1], 27 + j, {"tp": t1})
         c.start()
         near_n.append(c)
+    grad_up(QR)
     near_o = remote(npart.at[:, blk(t1), :], nrb1.at[1], 30, {"tp": t1})
     near_o.start()
+
+    far_n = []
+
+    def far_step(j):
+        k0, k1 = nsplit[j]
+        near_n[j].wait_recv()
+        nsb[k0:k1] = (npart[k0:k1, blk(t2), :].astype(F32) + nrb1[0, k0:k1].astype(F32)).astype(BF16)
+
+    def far_send(j):
+        k0, k1 = nsplit[j]
+        c = remote(nsb.at[k0:k1], nrb2.at[k0:k1], 41 + j, {"tp": t2})
+        c.start()
+        far_n.append(c)
+
+    far_step(0)
+    ex_up1 = remote(gup.at[:, rows_of(odp, QR), :], gup_rb.at[:, QR:2 * QR, :], 36, {"dp": odp})
+    ex_up1.start()
+    far_step(1)
+    far_send(0)
+    far_step(2)
+    far_send(1)
     ex_up0.wait_recv()
     gfin[:, rows_of(dp, 0), :] = (gup[:, rows_of(dp, 0), :] + gup_rb[:, 0:QR, :]).astype(BF16)
+    far_send(2)
+
+    s3 = jnp.zeros((ch, nat), F32)
     for k in range(COEFS):
         rf = npart[k].astype(F32) * gcol[degree_of(k)]
         if k == 0:
@@ -331,29 +366,6 @@
     st_snd[...] = jnp.concatenate([st0, st1, st2, jnp.zeros((5, nat), F32)], axis=0)
     bk_up0 = remote(gfin.at[:, rows_of(dp, 0), :], gfin.at[:, rows_of(dp, 0), :], 35, {"dp": odp})
     bk_up0.start()
-
-    far_n = []
-
-    def far_step(j):
-        k0, k1 = nsplit[j]
-        near_n[j].wait_recv()
-        nsb[k0:k1] = (npart[k0:k1, blk(t2), :].astype(F32) + nrb1[0, k0:k1].astype(F32)).astype(BF16)
-
-    def far_send(j):
-        k0, k1 = nsplit[j]
-        c = remote(nsb.at[k0:k1], nrb2.at[k0:k1], 41 + j, {"tp": t2})
-        c.start()
-        far_n.append(c)
-
-    far_step(0)
-    grad_up(None, QR)
-    far_send(0)
-    ex_up1 = remote(gup.at[:, rows_of(odp, QR), :], gup_rb.at[:, QR:2 * QR, :], 36, {"dp": odp})
-    ex_up1.start()
-    far_step(1)
-    far_step(2)
-    far_send(1)
-    far_send(2)
     ssend = []
     for j, dev in enumerate((t1, t2, t3)):
         c = remote(st_snd, st_all.at[j], 37 + j, {"tp": dev})
@@ -429,7 +441,7 @@
             scratch_shapes=[
                 full, full, full, full, full, full, full,
                 pltpu.VMEM((65 * YSTRIDE, 128), F32), pltpu.VMEM((65 * YSTRIDE, 128), F32),
-                pltpu.VMEM((KPAD * 136, 128), F32), pltpu.VMEM((65 * pp, 256), BF16),
+                pltpu.VMEM((KPAD * 136, 128), F32), pltpu.VMEM((64 * pp, 256), F32),
                 pltpu.VMEM(gain_loc.shape, F32), pltpu.VMEM((8, 128), F32), pltpu.VMEM((3, 8, 128), F32), sq(5, F32),
                 sq(5, BF16), pltpu.VMEM((128, 128), BF16), sq(5, BF16), sq(5, BF16), pltpu.VMEM((128, 128), BF16), sq(5, BF16),
                 pltpu.VMEM(to_grid.shape, F32), pltpu.VMEM(from_grid.shape[::-1], F32),

time: 49.1 us -> 47.1 us (0.959)
  Pallas kernels: 48.4 us -> 46.4 us
    pallas_call x1, Pallas kernels: 47.5 us -> 45.4 us  [local_step(): pl.pallas_call(functools.partial(kernel, tp_size, grid_pts), out_shape=tu...]
where the time goes in v4:
time: 47.1 us; the launch traced here: 47 us
  Pallas kernels  46.4 us (99%)
  between operations  0.64 us (1%)
    pallas_call x1, Pallas kernels, local_step(): pl.pallas_call(functools.partial(kernel, tp_size, grid_pts), out_shape=tu...  45.4 us

profile of v4, /device:TPU:0, one launch (start us, length us, event | category | flops | bytes accessed | tf_op | source)
XLA Modules:
  0.0 47.0 jit_solution(5751621998650285329)
XLA Ops:
  0.6 45.4 %shard_map.119 = (bf16[25,32,128]{2,1,0:T(8,128)(2,1)S(1)}, bf16[25,32,128]{2,1,0:T(8,128)(2,1)S(1)}, bf16[5,128,128]{2,1,0:T(8,128)(2,1)S(1)}, bf16[128,128]{1,0:T(8,128)(2,1)S(1)}, bf16[5,128,128]{2,1,0:T(8,128)(2,1)S(1)}) custom-call(bf16[25,32,128]{2,1,0:T(8,128)(2,1)} %bitcast.5, f32[5,32]{1,0:T(8,128)} %gain_hbm.1, bf16[5,128,128]{2,1,0:T(8,128)(2,1)} %up_hbm.1, ...), custom_call_target="tpu_custom_call" | custom-call | tf_op jit(solution)/shard_map/pallas_call | solution.py:436
  46.1 0.9 %shard_map.120 = (bf16[25,32,128]{2,1,0:T(8,128)(2,1)}, bf16[25,32,128]{2,1,0:T(8,128)(2,1)}, bf16[5,128,128]{2,1,0:T(8,128)(2,1)}, bf16[128,128]{1,0:T(8,128)(2,1)}, bf16[5,128,128]{2,1,0:T(8,128)(2,1)}) custom-call(bf16[25,32,128]{2,1,0:T(8,128)(2,1)S(1)} %get-tuple-element.15.a, bf16[25,32,128]{2,1,0:T(8,128)(2,1)S(1)} %get-tuple-element.16.b, ...), custom_call_target="tpu_custom_call" | custom-call | tf_op jit(solution)/shard_map/pallas_call | solution.py:458

commit v5 on v4

--- a/solution.py
+++ b/solution.py
@@ -62,9 +62,9 @@
         return pltpu.make_async_remote_copy(src_ref=src, dst_ref=dst, send_sem=snd_sem.at[i], recv_sem=rcv_sem.at[i],
                                             device_id=dev, device_id_type=MESH)
 
+    c_gain = local(gain_hbm, gain_in, 0)
     ksplit = ((0, 7), (7, 13), (13, 19), (19, 25))
     c_x = [local(x_hbm.at[k0:k1], xg.at[k0:k1, blk(t), :], 7 + j) for j, (k0, k1) in enumerate(ksplit)]
-    c_gain = local(gain_hbm, gain_in, 0)
     c_tog = local(tog_hbm, tog, 2)
     c_frg = local(frg_hbm, frg, 3)
     c_up = local(up_hbm, up, 4)
@@ -75,7 +75,17 @@
     barrier = pltpu.get_barrier_semaphore()
     for dev in ({"tp": t1}, {"tp": t2}, {"tp": t3}, {"dp": odp}):
         pl.semaphore_signal(barrier, inc=1, device_id=dev, device_id_type=MESH)
+    c_gain.wait()
+    gain_snd[...] = jnp.zeros_like(gain_snd)
+    gain_snd[0:5, 0:cl] = gain_in[...]
+    placed = pltpu.roll(gain_snd[...], t * cl, 1)
+    gain_snd[...] = placed
     pl.semaphore_wait(barrier, 4)
+    gsend = []
+    for j, dev in enumerate((t1, t2, t3)):
+        c = remote(gain_snd, gain_all.at[j], 20 + j, {"tp": dev})
+        c.start()
+        gsend.append(c)
 
     def gather_start(dst, base, ready=None):
         far = []
@@ -96,23 +106,14 @@
             c = remote(dst.at[k0:k1, blk(t2), :], dst.at[k0:k1, blk(t2), :], base + 5 + j, {"tp": t1})
             c.start()
             fwd.append(c)
+        return fwd
+
+    def gather_wait(near, fwd):
         near.wait_recv()
         for c in fwd:
             c.wait_recv()
-        return fwd
 
     far_x, near_x = gather_start(xg, 0, c_x)
-
-    gain_snd[...] = jnp.zeros_like(gain_snd)
-    c_gain.wait()
-    gain_snd[0:5, 0:cl] = gain_in[...]
-    placed = pltpu.roll(gain_snd[...], t * cl, 1)
-    gain_snd[...] = placed
-    gsend = []
-    for j, dev in enumerate((t1, t2, t3)):
-        c = remote(gain_snd, gain_all.at[j], 20 + j, {"tp": dev})
-        c.start()
-        gsend.append(c)
 
     c_tog.wait()
     c_frg.wait()
@@ -144,6 +145,7 @@
         gcol[l] = jnp.broadcast_to(gain_full[l:l + 1, :], (ch, ch)).T
 
     fwd_x = gather_finish(far_x, near_x, xg, 0)
+    gather_wait(near_x, fwd_x)
     for c in far_x:
         c.wait_send()
     c_g.wait()
@@ -220,7 +222,9 @@
             stage_s(p, gbuf[j % 2], sbuf[j % 2])
         return carry
 
-    lax.fori_loop(0, 64 // UNROLL, fwd_body, 0)
+    lax.fori_loop(0, 50 // UNROLL, fwd_body, 0)
+    fwd_g = gather_finish(far_g, near_g, gg, 10)
+    lax.fori_loop(50 // UNROLL, 64 // UNROLL, fwd_body, 0)
     stage_z(63, sbuf[1], ft)
 
     for k in range(1, COEFS):
@@ -238,7 +242,7 @@
 
     near_d = scatter_near(dpart, rb1, 23)
 
-    fwd_g = gather_finish(far_g, near_g, gg, 10)
+    gather_wait(near_g, fwd_g)
     spread(lambda k: gg[k], lambda l: down[l])
     dm0 = rows_dot(down[0], gg[0]).astype(BF16).astype(F32)
     a_h = amat[...].astype(F32) * 0.5
@@ -248,15 +252,11 @@
     for l in range(5):
         gdn[l] = over_degree(lambda k: mb[k], lambda k: gg[k], l)
     gdn[5] = lanes_dot(da, xn[0])
-    near_d[0].wait_recv()
-    sb[...] = (dpart[:, blk(t2), :].astype(F32) + rb1[0].astype(F32)).astype(BF16)
     half = 64
     mine = pl.ds(pl.multiple_of(dp * half, half), half)
     theirs = pl.ds(pl.multiple_of(odp * half, half), half)
     ex_dn = remote(gdn.at[:, theirs, :], gdn_rb, 26, {"dp": odp})
     ex_dn.start()
-    far_d = remote(sb, rb2, 25, {"tp": t2})
-    far_d.start()
 
     def stage_g(p, dst):
         dst[...] = rows_dot(fmat[...], pair(p)).astype(BF16)
@@ -291,8 +291,13 @@
         return pl.ds(pl.multiple_of(d * half + lo, QR), QR)
 
     mid_steps = (QR + 2) // UNROLL
-    late_steps = 52 // UNROLL
-    lax.fori_loop(0, mid_steps, bwd_body, 0)
+    late_steps = 56 // UNROLL
+    lax.fori_loop(0, 6 // UNROLL, bwd_body, 0)
+    near_d[0].wait_recv()
+    sb[...] = (dpart[:, blk(t2), :].astype(F32) + rb1[0].astype(F32)).astype(BF16)
+    far_d = remote(sb, rb2, 25, {"tp": t2})
+    far_d.start()
+    lax.fori_loop(6 // UNROLL, mid_steps, bwd_body, 0)
 
     grad_up(0)
     ex_up0 = remote(gup.at[:, rows_of(odp, 0), :], gup_rb.at[:, 0:QR, :], 33, {"dp": odp})

time: 47.1 us -> 44.7 us (0.949)
  Pallas kernels: 46.4 us -> 43.9 us
    pallas_call x1, Pallas kernels: 45.4 us -> 43 us  [local_step(): pl.pallas_call(functools.partial(kernel, tp_size, grid_pts), out_shape=tu...]
where the time goes in v5:
time: 44.7 us; the launch traced here: 44.6 us
  Pallas kernels  43.9 us (98%)
  between operations  0.64 us (1%)
    pallas_call x1, Pallas kernels, local_step(): pl.pallas_call(functools.partial(kernel, tp_size, grid_pts), out_shape=tu...  43 us
    pallas_call x1, Pallas kernels, local_step(): pl.pallas_call(flush, out_shape=tuple((jax.ShapeDtypeStruct(sh, BF16) for...  0.91 us

profile of v5, /device:TPU:0, one launch (start us, length us, event | category | flops | bytes accessed | tf_op | source)
XLA Modules:
  0.0 44.6 jit_solution(1626002463485109012)
XLA Ops:
  0.6 43.0 %shard_map.119 = (bf16[25,32,128]{2,1,0:T(8,128)(2,1)S(1)}, bf16[25,32,128]{2,1,0:T(8,128)(2,1)S(1)}, bf16[5,128,128]{2,1,0:T(8,128)(2,1)S(1)}, bf16[128,128]{1,0:T(8,128)(2,1)S(1)}, bf16[5,128,128]{2,1,0:T(8,128)(2,1)S(1)}) custom-call(bf16[25,32,128]{2,1,0:T(8,128)(2,1)} %bitcast.5, f32[5,32]{1,0:T(8,128)} %gain_hbm.1, bf16[5,128,128]{2,1,0:T(8,128)(2,1)} %up_hbm.1, ...), custom_call_target="tpu_custom_call" | custom-call | tf_op jit(solution)/shard_map/pallas_call | solution.py:441
  43.6 0.9 %shard_map.120 = (bf16[25,32,128]{2,1,0:T(8,128)(2,1)}, bf16[25,32,128]{2,1,0:T(8,128)(2,1)}, bf16[5,128,128]{2,1,0:T(8,128)(2,1)}, bf16[128,128]{1,0:T(8,128)(2,1)}, bf16[5,128,128]{2,1,0:T(8,128)(2,1)}) custom-call(bf16[25,32,128]{2,1,0:T(8,128)(2,1)S(1)} %get-tuple-element.15.a, bf16[25,32,128]{2,1,0:T(8,128)(2,1)S(1)} %get-tuple-element.16.b, ...), custom_call_target="tpu_custom_call" | custom-call | tf_op jit(solution)/shard_map/pallas_call | solution.py:463

commit v6 on v5

--- a/solution.py
+++ b/solution.py
@@ -14,7 +14,7 @@
 COEFS = 25
 KPAD = 32
 YSTRIDE = 40
-UNROLL = 2
+UNROLL = 4
 QR = 32
 
 
@@ -35,9 +35,9 @@
            xg, gg, xn, mb, dyb, dpart, npart, ya, yb, zs, hs,
            gain_in, gain_snd, gain_all, gcol, up, gate, down, upt, gatet, downt,
            tog, frg, tt, tmat, fmat, ft, rb1, sb, rb2, nrb1, nsb, nrb2,
-           st_snd, st_all, gdn, gdn_rb, gup, gup_rb, gfin, gfin_dn, amat, sbuf0, sbuf1, gbuf0, gbuf1,
+           st_snd, st_all, gdn, gdn_rb, gup, gup_rb, gfin, gfin_dn, amat, sbuf0, sbuf1, sbuf2, sbuf3, gbuf0, gbuf1, gbuf2, gbuf3,
            loc_sem, snd_sem, rcv_sem):
-    sbuf, gbuf = (sbuf0, sbuf1), (gbuf0, gbuf1)
+    sbuf, gbuf = (sbuf0, sbuf1, sbuf2, sbuf3), (gbuf0, gbuf1, gbuf2, gbuf3)
     dp = lax.axis_index("dp")
     t = lax.axis_index("tp")
     core = lax.rem(t, 2)
@@ -213,19 +213,23 @@
         put(p, rows_dot(lhs[:, 0:pp], src[...]))
 
     stage_u(0, gbuf[0])
+    stage_u(1, gbuf[1])
 
     def fwd_body(it, carry):
-        for j in range(UNROLL):
-            p = it * UNROLL + j
-            stage_z(jnp.maximum(p - 1, 0), sbuf[(j + 1) % 2], ft)
-            stage_u(p + 1, gbuf[(j + 1) % 2])
-            stage_s(p, gbuf[j % 2], sbuf[j % 2])
+        for half_step in range(2):
+            p = it * UNROLL + 2 * half_step
+            now, other = 2 * (half_step % 2), 2 * ((half_step + 1) % 2)
+            for j in range(2):
+                stage_z(jnp.maximum(p + j - 2, 0), sbuf[other + j], ft)
+                stage_u(p + j + 2, gbuf[other + j])
+                stage_s(p + j, gbuf[now + j], sbuf[now + j])
         return carry
 
-    lax.fori_loop(0, 50 // UNROLL, fwd_body, 0)
+    lax.fori_loop(0, 48 // UNROLL, fwd_body, 0)
     fwd_g = gather_finish(far_g, near_g, gg, 10)
-    lax.fori_loop(50 // UNROLL, 64 // UNROLL, fwd_body, 0)
-    stage_z(63, sbuf[1], ft)
+    lax.fori_loop(48 // UNROLL, 64 // UNROLL, fwd_body, 0)
+    stage_z(62, sbuf[2], ft)
+    stage_z(63, sbuf[3], ft)
 
     for k in range(1, COEFS):
         mb[k] = zs[k * 136:k * 136 + 128, :].astype(BF16)
@@ -266,13 +270,16 @@
         dst[...] = (src[...].astype(F32) * gp).astype(BF16)
 
     stage_g(0, gbuf[0])
+    stage_g(1, gbuf[1])
 
     def bwd_body(it, carry):
-        for j in range(UNROLL):
-            p = it * UNROLL + j
-            stage_z(jnp.maximum(p - 1, 0), sbuf[(j + 1) % 2], tmat)
-            stage_g(p + 1, gbuf[(j + 1) % 2])
-            stage_e(p, gbuf[j % 2], sbuf[j % 2])
+        for half_step in range(2):
+            p = it * UNROLL + 2 * half_step
+            now, other = 2 * (half_step % 2), 2 * ((half_step + 1) % 2)
+            for j in range(2):
+                stage_z(jnp.maximum(p + j - 2, 0), sbuf[other + j], tmat)
+                stage_g(p + j + 2, gbuf[other + j])
+                stage_e(p + j, gbuf[now + j], sbuf[now + j])
         return carry
 
     def grad_up(lo):
@@ -290,14 +297,14 @@
     def rows_of(d, lo):
         return pl.ds(pl.multiple_of(d * half + lo, QR), QR)
 
-    mid_steps = (QR + 2) // UNROLL
+    mid_steps = (QR + 4) // UNROLL
     late_steps = 56 // UNROLL
-    lax.fori_loop(0, 6 // UNROLL, bwd_body, 0)
+    lax.fori_loop(0, 8 // UNROLL, bwd_body, 0)
     near_d[0].wait_recv()
     sb[...] = (dpart[:, blk(t2), :].astype(F32) + rb1[0].astype(F32)).astype(BF16)
     far_d = remote(sb, rb2, 25, {"tp": t2})
     far_d.start()
-    lax.fori_loop(6 // UNROLL, mid_steps, bwd_body, 0)
+    lax.fori_loop(8 // UNROLL, mid_steps, bwd_body, 0)
 
     grad_up(0)
     ex_up0 = remote(gup.at[:, rows_of(odp, 0), :], gup_rb.at[:, 0:QR, :], 33, {"dp": odp})
@@ -315,7 +322,8 @@
     bk_dn.start()
 
     lax.fori_loop(late_steps, 64 // UNROLL, bwd_body, 0)
-    stage_z(63, sbuf[1], tmat)
+    stage_z(62, sbuf[2], tmat)
+    stage_z(63, sbuf[3], tmat)
 
     def full_dy(k):
         return jnp.concatenate([dyb[k, 0:QR, :], zs[k * 136 + QR:k * 136 + 64, :].astype(BF16),
@@ -445,7 +453,7 @@
             out_specs=[vmem] * 5,
             scratch_shapes=[
                 full, full, full, full, full, full, full,
-                pltpu.VMEM((65 * YSTRIDE, 128), F32), pltpu.VMEM((65 * YSTRIDE, 128), F32),
+                pltpu.VMEM((66 * YSTRIDE, 128), F32), pltpu.VMEM((66 * YSTRIDE, 128), F32),
                 pltpu.VMEM((KPAD * 136, 128), F32), pltpu.VMEM((64 * pp, 256), F32),
                 pltpu.VMEM(gain_loc.shape, F32), pltpu.VMEM((8, 128), F32), pltpu.VMEM((3, 8, 128), F32), sq(5, F32),
                 sq(5, BF16), pltpu.VMEM((128, 128), BF16), sq(5, BF16), sq(5, BF16), pltpu.VMEM((128, 128), BF16), sq(5, BF16),
@@ -455,6 +463,7 @@
                 pltpu.VMEM((8, 128), F32), pltpu.VMEM((3, 8, 128), F32),
                 sq(6, F32), pltpu.VMEM((6, 64, 128), F32), sq(5, F32), pltpu.VMEM((5, 64, 128), F32), sq(5, BF16), sq(6, BF16),
                 pltpu.VMEM((128, nat), BF16),
+                pltpu.VMEM((pp, 256), BF16), pltpu.VMEM((pp, 256), BF16), pltpu.VMEM((pp, 256), BF16), pltpu.VMEM((pp, 256), BF16),
                 pltpu.VMEM((pp, 256), BF16), pltpu.VMEM((pp, 256), BF16), pltpu.VMEM((pp, 256), BF16), pltpu.VMEM((pp, 256), BF16),
                 pltpu.SemaphoreType.DMA((12,)), pltpu.SemaphoreType.DMA((44,)), pltpu.SemaphoreType.DMA((44,)),
             ],

time: 44.7 us -> 43.8 us (0.980)
  Pallas kernels: 43.9 us -> 43 us
    pallas_call x1, Pallas kernels: 43 us -> 42.1 us  [local_step(): pl.pallas_call(functools.partial(kernel, tp_size, grid_pts), out_shape=tu...]
where the time goes in v6:
time: 43.8 us; the launch traced here: 43.7 us
  Pallas kernels  43 us (98%)
  between operations  0.64 us (1%)
    pallas_call x1, Pallas kernels, local_step(): pl.pallas_call(functools.partial(kernel, tp_size, grid_pts), out_shape=tu...  42.1 us
    pallas_call x1, Pallas kernels, local_step(): pl.pallas_call(flush, out_shape=tuple((jax.ShapeDtypeStruct(sh, BF16) for...  0.91 us

profile of v6, /device:TPU:0, one launch (start us, length us, event | category | flops | bytes accessed | tf_op | source)
XLA Modules:
  0.0 43.7 jit_solution(17611282710025063285)
XLA Ops:
  0.6 42.1 %shard_map.119 = (bf16[25,32,128]{2,1,0:T(8,128)(2,1)S(1)}, bf16[25,32,128]{2,1,0:T(8,128)(2,1)S(1)}, bf16[5,128,128]{2,1,0:T(8,128)(2,1)S(1)}, bf16[128,128]{1,0:T(8,128)(2,1)S(1)}, bf16[5,128,128]{2,1,0:T(8,128)(2,1)S(1)}) custom-call(bf16[25,32,128]{2,1,0:T(8,128)(2,1)} %bitcast.5, f32[5,32]{1,0:T(8,128)} %gain_hbm.1, bf16[5,128,128]{2,1,0:T(8,128)(2,1)} %up_hbm.1, ...), custom_call_target="tpu_custom_call" | custom-call | tf_op jit(solution)/shard_map/pallas_call | solution.py:449
  42.8 0.9 %shard_map.120 = (bf16[25,32,128]{2,1,0:T(8,128)(2,1)}, bf16[25,32,128]{2,1,0:T(8,128)(2,1)}, bf16[5,128,128]{2,1,0:T(8,128)(2,1)}, bf16[128,128]{1,0:T(8,128)(2,1)}, bf16[5,128,128]{2,1,0:T(8,128)(2,1)}) custom-call(bf16[25,32,128]{2,1,0:T(8,128)(2,1)S(1)} %get-tuple-element.15.a, bf16[25,32,128]{2,1,0:T(8,128)(2,1)S(1)} %get-tuple-element.16.b, ...), custom_call_target="tpu_custom_call" | custom-call | tf_op jit(solution)/shard_map/pallas_call | solution.py:472

commit v7 on v6

--- a/solution.py
+++ b/solution.py
@@ -63,7 +63,7 @@
                                             device_id=dev, device_id_type=MESH)
 
     c_gain = local(gain_hbm, gain_in, 0)
-    ksplit = ((0, 7), (7, 13), (13, 19), (19, 25))
+    ksplit = ((0, 8), (8, 15), (15, 22), (22, 25))
     c_x = [local(x_hbm.at[k0:k1], xg.at[k0:k1, blk(t), :], 7 + j) for j, (k0, k1) in enumerate(ksplit)]
     c_tog = local(tog_hbm, tog, 2)
     c_frg = local(frg_hbm, frg, 3)
@@ -95,23 +95,35 @@
             c = remote(dst.at[k0:k1, blk(t), :], dst.at[k0:k1, blk(t), :], base + j, {"tp": t2})
             c.start()
             far.append(c)
+        k0, k1 = ksplit[-1]
+        c = remote(dst.at[k0:k1, blk(t), :], dst.at[k0:k1, blk(t), :], base + 8, {"tp": t3})
+        c.start()
+        far.append(c)
         near = remote(dst.at[:, blk(t), :], dst.at[:, blk(t), :], base + 4, {"tp": t1})
         near.start()
         return far, near
 
-    def gather_finish(far, near, dst, base):
+    def gather_finish(far, near, dst, base, step=None):
         fwd = []
-        for j, (k0, k1) in enumerate(ksplit):
+        for j, (k0, k1) in enumerate(ksplit[:-1]):
             far[j].wait_recv()
             c = remote(dst.at[k0:k1, blk(t2), :], dst.at[k0:k1, blk(t2), :], base + 5 + j, {"tp": t1})
             c.start()
             fwd.append(c)
+            if step and j == 0:
+                near.wait_recv()
+                step((t, t1), 0, COEFS)
+            if step and j > 0:
+                fwd[j - 1].wait_recv()
+                step((t2, t3), *ksplit[j - 1])
         return fwd
 
-    def gather_wait(near, fwd):
+    def gather_wait(far, near, fwd):
         near.wait_recv()
         for c in fwd:
             c.wait_recv()
+        far[-2].wait_recv()
+        far[-1].wait_recv()
 
     far_x, near_x = gather_start(xg, 0, c_x)
 
@@ -144,8 +156,20 @@
     for l in range(5):
         gcol[l] = jnp.broadcast_to(gain_full[l:l + 1, :], (ch, ch)).T
 
-    fwd_x = gather_finish(far_x, near_x, xg, 0)
-    gather_wait(near_x, fwd_x)
+    sums = [jnp.zeros((cl, nat), F32)]
+
+    def square_step(blocks, k0, k1):
+        for k in range(max(k0, 1), k1):
+            for i in blocks:
+                v = xg[k, blk(i), :].astype(F32)
+                sums[0] = sums[0] + v * v
+
+    fwd_x = gather_finish(far_x, near_x, xg, 0, square_step)
+    fwd_x[-1].wait_recv()
+    square_step((t2, t3), *ksplit[2])
+    far_x[-2].wait_recv()
+    far_x[-1].wait_recv()
+    square_step((t2, t3), *ksplit[3])
     for c in far_x:
         c.wait_send()
     c_g.wait()
@@ -156,11 +180,7 @@
     cent = x0 - mean_s
     inv_s = lax.rsqrt(jnp.sum(cent * cent, axis=0, keepdims=True) / ch + NORM_EPS)
     hat_s = cent * inv_s
-    acc = jnp.zeros((ch, nat), F32)
-    for k in range(1, COEFS):
-        v = xg[k].astype(F32)
-        acc = acc + v * v
-    inv_v = lax.rsqrt(jnp.sum(acc, axis=0, keepdims=True) / (ch * (COEFS - 1)) + NORM_EPS)
+    inv_v = lax.rsqrt(jnp.sum(sums[0], axis=0, keepdims=True) / (ch * (COEFS - 1)) + NORM_EPS)
     xn[0] = (hat_s * gcol[0]).astype(BF16)
     for k in range(1, COEFS):
         xn[k] = (xg[k].astype(F32) * inv_v * gcol[degree_of(k)]).astype(BF16)
@@ -246,7 +266,7 @@
 
     near_d = scatter_near(dpart, rb1, 23)
 
-    gather_wait(near_g, fwd_g)
+    gather_wait(far_g, near_g, fwd_g)
     spread(lambda k: gg[k], lambda l: down[l])
     dm0 = rows_dot(down[0], gg[0]).astype(BF16).astype(F32)
     a_h = amat[...].astype(F32) * 0.5
@@ -298,32 +318,22 @@
         return pl.ds(pl.multiple_of(d * half + lo, QR), QR)
 
     mid_steps = (QR + 4) // UNROLL
-    late_steps = 56 // UNROLL
-    lax.fori_loop(0, 8 // UNROLL, bwd_body, 0)
+    lax.fori_loop(0, 4 // UNROLL, bwd_body, 0)
     near_d[0].wait_recv()
     sb[...] = (dpart[:, blk(t2), :].astype(F32) + rb1[0].astype(F32)).astype(BF16)
     far_d = remote(sb, rb2, 25, {"tp": t2})
     far_d.start()
-    lax.fori_loop(8 // UNROLL, mid_steps, bwd_body, 0)
+    lax.fori_loop(4 // UNROLL, mid_steps, bwd_body, 0)
 
     grad_up(0)
     ex_up0 = remote(gup.at[:, rows_of(odp, 0), :], gup_rb.at[:, 0:QR, :], 33, {"dp": odp})
     ex_up0.start()
 
-    lax.fori_loop(mid_steps, late_steps, bwd_body, 0)
-
+    lax.fori_loop(mid_steps, 64 // UNROLL, bwd_body, 0)
+    stage_z(62, sbuf[2], tmat)
+    stage_z(63, sbuf[3], tmat)
     ex_dn.wait_recv()
     gfin_dn[:, mine, :] = (gdn[:, mine, :] + gdn_rb[...]).astype(BF16)
-    near_d[1].wait_recv()
-    far_d.wait_recv()
-    own = dpart[:, blk(t), :].astype(F32) + rb1[1].astype(F32) + rb2[...].astype(F32)
-    out_ref[...] = (xg[:, blk(t), :].astype(F32) + own).astype(BF16)
-    bk_dn = remote(gfin_dn.at[:, mine, :], gfin_dn.at[:, mine, :], 34, {"dp": odp})
-    bk_dn.start()
-
-    lax.fori_loop(late_steps, 64 // UNROLL, bwd_body, 0)
-    stage_z(62, sbuf[2], tmat)
-    stage_z(63, sbuf[3], tmat)
 
     def full_dy(k):
         return jnp.concatenate([dyb[k, 0:QR, :], zs[k * 136 + QR:k * 136 + 64, :].astype(BF16),
@@ -339,6 +349,9 @@
         c = remote(npart.at[k0:k1, blk(t3), :], nrb1.at[0, k0:k1], 27 + j, {"tp": t1})
         c.start()
         near_n.append(c)
+        if j == 0:
+            bk_dn = remote(gfin_dn.at[:, mine, :], gfin_dn.at[:, mine, :], 34, {"dp": odp})
+            bk_dn.start()
     grad_up(QR)
     near_o = remote(npart.at[:, blk(t1), :], nrb1.at[1], 30, {"tp": t1})
     near_o.start()
@@ -367,6 +380,10 @@
     gfin[:, rows_of(dp, 0), :] = (gup[:, rows_of(dp, 0), :] + gup_rb[:, 0:QR, :]).astype(BF16)
     far_send(2)
 
+    near_d[1].wait_recv()
+    far_d.wait_recv()
+    own = dpart[:, blk(t), :].astype(F32) + rb1[1].astype(F32) + rb2[...].astype(F32)
+    out_ref[...] = (xg[:, blk(t), :].astype(F32) + own).astype(BF16)
     s3 = jnp.zeros((ch, nat), F32)
     for k in range(COEFS):
         rf = npart[k].astype(F32) * gcol[degree_of(k)]

time: 43.8 us -> 42.6 us (0.973)
  Pallas kernels: 43 us -> 41.9 us
    pallas_call x1, Pallas kernels: 42.1 us -> 41 us  [local_step(): pl.pallas_call(functools.partial(kernel, tp_size, grid_pts), out_shape=tu...]
where the time goes in v7:
time: 42.6 us; the launch traced here: 42.5 us
  Pallas kernels  41.9 us (98%)
  between operations  0.64 us (2%)
    pallas_call x1, Pallas kernels, local_step(): pl.pallas_call(functools.partial(kernel, tp_size, grid_pts), out_shape=tu...  41 us
    pallas_call x1, Pallas kernels, local_step(): pl.pallas_call(flush, out_shape=tuple((jax.ShapeDtypeStruct(sh, BF16) for...  0.91 us

profile of v7, /device:TPU:0, one launch (start us, length us, event | category | flops | bytes accessed | tf_op | source)
XLA Modules:
  0.0 42.5 jit_solution(15020358192354571387)
XLA Ops:
  0.6 41.0 %shard_map.119 = (bf16[25,32,128]{2,1,0:T(8,128)(2,1)S(1)}, bf16[25,32,128]{2,1,0:T(8,128)(2,1)S(1)}, bf16[5,128,128]{2,1,0:T(8,128)(2,1)S(1)}, bf16[128,128]{1,0:T(8,128)(2,1)S(1)}, bf16[5,128,128]{2,1,0:T(8,128)(2,1)S(1)}) custom-call(bf16[25,32,128]{2,1,0:T(8,128)(2,1)} %bitcast.5, f32[5,32]{1,0:T(8,128)} %gain_hbm.1, bf16[5,128,128]{2,1,0:T(8,128)(2,1)} %up_hbm.1, ...), custom_call_target="tpu_custom_call" | custom-call | tf_op jit(solution)/shard_map/pallas_call | solution.py:466
  41.6 0.9 %shard_map.120 = (bf16[25,32,128]{2,1,0:T(8,128)(2,1)}, bf16[25,32,128]{2,1,0:T(8,128)(2,1)}, bf16[5,128,128]{2,1,0:T(8,128)(2,1)}, bf16[128,128]{1,0:T(8,128)(2,1)}, bf16[5,128,128]{2,1,0:T(8,128)(2,1)}) custom-call(bf16[25,32,128]{2,1,0:T(8,128)(2,1)S(1)} %get-tuple-element.15.a, bf16[25,32,128]{2,1,0:T(8,128)(2,1)S(1)} %get-tuple-element.16.b, ...), custom_call_target="tpu_custom_call" | custom-call | tf_op jit(solution)/shard_map/pallas_call | solution.py:489

commit v8 on v7

--- a/solution.py
+++ b/solution.py
@@ -15,7 +15,7 @@
 KPAD = 32
 YSTRIDE = 40
 UNROLL = 4
-QR = 32
+QR = 48
 
 
 def degree_of(k):
@@ -302,20 +302,22 @@
                 stage_e(p + j, gbuf[now + j], sbuf[now + j])
         return carry
 
-    def grad_up(lo):
-        def dy(k):
-            return jnp.concatenate([dyb[k, lo:lo + QR, :], dyb[k, 64 + lo:64 + lo + QR, :]], axis=0)
-
+    def keep_dy(lo, n):
         for k in range(COEFS):
             for o in (lo, 64 + lo):
-                dyb[k, o:o + QR, :] = zs[k * 136 + o:k * 136 + o + QR, :].astype(BF16)
+                dyb[k, o:o + n, :] = zs[k * 136 + o:k * 136 + o + n, :].astype(BF16)
+
+    def grad_up(lo, n):
+        def dy(k):
+            return jnp.concatenate([dyb[k, lo:lo + n, :], dyb[k, 64 + lo:64 + lo + n, :]], axis=0)
+
         for l in range(5):
             acc = over_degree(dy, lambda k: xn[k], l)
-            gup[l, lo:lo + QR, :] = acc[0:QR]
-            gup[l, 64 + lo:64 + lo + QR, :] = acc[QR:2 * QR]
+            gup[l, lo:lo + n, :] = acc[0:n]
+            gup[l, 64 + lo:64 + lo + n, :] = acc[n:2 * n]
 
     def rows_of(d, lo):
-        return pl.ds(pl.multiple_of(d * half + lo, QR), QR)
+        return pl.ds(pl.multiple_of(d * half + lo, 16), half - QR if lo else QR)
 
     mid_steps = (QR + 4) // UNROLL
     lax.fori_loop(0, 4 // UNROLL, bwd_body, 0)
@@ -325,15 +327,18 @@
     far_d.start()
     lax.fori_loop(4 // UNROLL, mid_steps, bwd_body, 0)
 
-    grad_up(0)
+    keep_dy(0, QR)
+    grad_up(0, QR)
     ex_up0 = remote(gup.at[:, rows_of(odp, 0), :], gup_rb.at[:, 0:QR, :], 33, {"dp": odp})
+    ex_dn.wait_recv()
+    gfin_dn[:, mine, :] = (gdn[:, mine, :] + gdn_rb[...]).astype(BF16)
     ex_up0.start()
+    bk_dn = remote(gfin_dn.at[:, mine, :], gfin_dn.at[:, mine, :], 34, {"dp": odp})
+    bk_dn.start()
 
     lax.fori_loop(mid_steps, 64 // UNROLL, bwd_body, 0)
     stage_z(62, sbuf[2], tmat)
     stage_z(63, sbuf[3], tmat)
-    ex_dn.wait_recv()
-    gfin_dn[:, mine, :] = (gdn[:, mine, :] + gdn_rb[...]).astype(BF16)
 
     def full_dy(k):
         return jnp.concatenate([dyb[k, 0:QR, :], zs[k * 136 + QR:k * 136 + 64, :].astype(BF16),
@@ -349,10 +354,6 @@
         c = remote(npart.at[k0:k1, blk(t3), :], nrb1.at[0, k0:k1], 27 + j, {"tp": t1})
         c.start()
         near_n.append(c)
-        if j == 0:
-            bk_dn = remote(gfin_dn.at[:, mine, :], gfin_dn.at[:, mine, :], 34, {"dp": odp})
-            bk_dn.start()
-    grad_up(QR)
     near_o = remote(npart.at[:, blk(t1), :], nrb1.at[1], 30, {"tp": t1})
     near_o.start()
 
@@ -370,20 +371,13 @@
         far_n.append(c)
 
     far_step(0)
-    ex_up1 = remote(gup.at[:, rows_of(odp, QR), :], gup_rb.at[:, QR:2 * QR, :], 36, {"dp": odp})
+    keep_dy(QR, half - QR)
+    far_send(0)
+    grad_up(QR, half - QR)
+    far_step(1)
+    far_step(2)
+    ex_up1 = remote(gup.at[:, rows_of(odp, QR), :], gup_rb.at[:, QR:64, :], 36, {"dp": odp})
     ex_up1.start()
-    far_step(1)
-    far_send(0)
-    far_step(2)
-    far_send(1)
-    ex_up0.wait_recv()
-    gfin[:, rows_of(dp, 0), :] = (gup[:, rows_of(dp, 0), :] + gup_rb[:, 0:QR, :]).astype(BF16)
-    far_send(2)
-
-    near_d[1].wait_recv()
-    far_d.wait_recv()
-    own = dpart[:, blk(t), :].astype(F32) + rb1[1].astype(F32) + rb2[...].astype(F32)
-    out_ref[...] = (xg[:, blk(t), :].astype(F32) + own).astype(BF16)
     s3 = jnp.zeros((ch, nat), F32)
     for k in range(COEFS):
         rf = npart[k].astype(F32) * gcol[degree_of(k)]
@@ -392,21 +386,30 @@
             st1 = jnp.sum(rf * hat_s, axis=0, keepdims=True)
         else:
             s3 = s3 + rf * xg[k].astype(F32)
+        if k == 4:
+            far_send(1)
     st2 = jnp.sum(s3, axis=0, keepdims=True)
     st_snd[...] = jnp.concatenate([st0, st1, st2, jnp.zeros((5, nat), F32)], axis=0)
-    bk_up0 = remote(gfin.at[:, rows_of(dp, 0), :], gfin.at[:, rows_of(dp, 0), :], 35, {"dp": odp})
-    bk_up0.start()
+    ex_up0.wait_recv()
+    gfin[:, rows_of(dp, 0), :] = (gup[:, rows_of(dp, 0), :] + gup_rb[:, 0:QR, :]).astype(BF16)
     ssend = []
     for j, dev in enumerate((t1, t2, t3)):
         c = remote(st_snd, st_all.at[j], 37 + j, {"tp": dev})
         c.start()
         ssend.append(c)
+    far_send(2)
+    near_d[1].wait_recv()
+    far_d.wait_recv()
+    own = dpart[:, blk(t), :].astype(F32) + rb1[1].astype(F32) + rb2[...].astype(F32)
+    out_ref[...] = (xg[:, blk(t), :].astype(F32) + own).astype(BF16)
+    bk_up0 = remote(gfin.at[:, rows_of(dp, 0), :], gfin.at[:, rows_of(dp, 0), :], 35, {"dp": odp})
+    bk_up0.start()
 
     bk_dn.wait_recv()
     ddown_ref[...] = gfin_dn[0:5]
     dgate_ref[...] = gfin_dn[5].astype(F32).T.astype(BF16)
     ex_up1.wait_recv()
-    gfin[:, rows_of(dp, QR), :] = (gup[:, rows_of(dp, QR), :] + gup_rb[:, QR:2 * QR, :]).astype(BF16)
+    gfin[:, rows_of(dp, QR), :] = (gup[:, rows_of(dp, QR), :] + gup_rb[:, QR:64, :]).astype(BF16)
     for c in ssend:
         c.wait_recv()
     stat = st_snd[...] + st_all[0] + st_all[1] + st_all[2]

time: 42.6 us -> 41.1 us (0.965)
  Pallas kernels: 41.9 us -> 40.3 us
    pallas_call x1, Pallas kernels: 41 us -> 39.4 us  [local_step(): pl.pallas_call(functools.partial(kernel, tp_size, grid_pts), out_shape=tu...]
where the time goes in v8:
time: 41.1 us; the launch traced here: 41 us
  Pallas kernels  40.3 us (98%)
  between operations  0.64 us (2%)
    pallas_call x1, Pallas kernels, local_step(): pl.pallas_call(functools.partial(kernel, tp_size, grid_pts), out_shape=tu...  39.4 us
    pallas_call x1, Pallas kernels, local_step(): pl.pallas_call(flush, out_shape=tuple((jax.ShapeDtypeStruct(sh, BF16) for...  0.91 us

profile of v8, /device:TPU:0, one launch (start us, length us, event | category | flops | bytes accessed | tf_op | source)
XLA Modules:
  0.0 41.0 jit_solution(876906752158506081)
XLA Ops:
  0.6 39.4 %shard_map.119 = (bf16[25,32,128]{2,1,0:T(8,128)(2,1)S(1)}, bf16[25,32,128]{2,1,0:T(8,128)(2,1)S(1)}, bf16[5,128,128]{2,1,0:T(8,128)(2,1)S(1)}, bf16[128,128]{1,0:T(8,128)(2,1)S(1)}, bf16[5,128,128]{2,1,0:T(8,128)(2,1)S(1)}) custom-call(bf16[25,32,128]{2,1,0:T(8,128)(2,1)} %bitcast.5, f32[5,32]{1,0:T(8,128)} %gain_hbm.1, bf16[5,128,128]{2,1,0:T(8,128)(2,1)} %up_hbm.1, ...), custom_call_target="tpu_custom_call" | custom-call | tf_op jit(solution)/shard_map/pallas_call | solution.py:469
  40.1 0.9 %shard_map.120 = (bf16[25,32,128]{2,1,0:T(8,128)(2,1)}, bf16[25,32,128]{2,1,0:T(8,128)(2,1)}, bf16[5,128,128]{2,1,0:T(8,128)(2,1)}, bf16[128,128]{1,0:T(8,128)(2,1)}, bf16[5,128,128]{2,1,0:T(8,128)(2,1)}) custom-call(bf16[25,32,128]{2,1,0:T(8,128)(2,1)S(1)} %get-tuple-element.15.a, bf16[25,32,128]{2,1,0:T(8,128)(2,1)S(1)} %get-tuple-element.16.b, ...), custom_call_target="tpu_custom_call" | custom-call | tf_op jit(solution)/shard_map/pallas_call | solution.py:492

commit v9 on v8

--- a/solution.py
+++ b/solution.py
@@ -248,8 +248,21 @@
     lax.fori_loop(0, 48 // UNROLL, fwd_body, 0)
     fwd_g = gather_finish(far_g, near_g, gg, 10)
     lax.fori_loop(48 // UNROLL, 64 // UNROLL, fwd_body, 0)
+    gather_wait(far_g, near_g, fwd_g)
     stage_z(62, sbuf[2], ft)
     stage_z(63, sbuf[3], ft)
+
+    def stage_g(p, dst):
+        dst[...] = rows_dot(fmat[...], pair(p)).astype(BF16)
+
+    spread(lambda k: gg[k], lambda l: down[l])
+    dm0 = rows_dot(down[0], gg[0]).astype(BF16).astype(F32)
+    a_h = amat[...].astype(F32) * 0.5
+    w_a = 1.0 + jnp.tanh(a_h)
+    da = (dm0 * (0.5 * w_a * (1.0 + a_h * (2.0 - w_a)))).astype(BF16)
+
+    stage_g(0, gbuf[0])
+    stage_g(1, gbuf[1])
 
     for k in range(1, COEFS):
         mb[k] = zs[k * 136:k * 136 + 128, :].astype(BF16)
@@ -265,13 +278,6 @@
         return cs
 
     near_d = scatter_near(dpart, rb1, 23)
-
-    gather_wait(far_g, near_g, fwd_g)
-    spread(lambda k: gg[k], lambda l: down[l])
-    dm0 = rows_dot(down[0], gg[0]).astype(BF16).astype(F32)
-    a_h = amat[...].astype(F32) * 0.5
-    w_a = 1.0 + jnp.tanh(a_h)
-    da = (dm0 * (0.5 * w_a * (1.0 + a_h * (2.0 - w_a)))).astype(BF16)
 
     for l in range(5):
         gdn[l] = over_degree(lambda k: mb[k], lambda k: gg[k], l)
@@ -282,15 +288,10 @@
     ex_dn = remote(gdn.at[:, theirs, :], gdn_rb, 26, {"dp": odp})
     ex_dn.start()
 
-    def stage_g(p, dst):
-        dst[...] = rows_dot(fmat[...], pair(p)).astype(BF16)
-
     def stage_e(p, src, dst):
         gp = hs[pl.ds(pl.multiple_of(p * pp, 16), pp), :]
         dst[...] = (src[...].astype(F32) * gp).astype(BF16)
 
-    stage_g(0, gbuf[0])
-    stage_g(1, gbuf[1])
 
     def bwd_body(it, carry):
         for half_step in range(2):
@@ -320,12 +321,12 @@
         return pl.ds(pl.multiple_of(d * half + lo, 16), half - QR if lo else QR)
 
     mid_steps = (QR + 4) // UNROLL
-    lax.fori_loop(0, 4 // UNROLL, bwd_body, 0)
+    lax.fori_loop(0, 12 // UNROLL, bwd_body, 0)
     near_d[0].wait_recv()
     sb[...] = (dpart[:, blk(t2), :].astype(F32) + rb1[0].astype(F32)).astype(BF16)
     far_d = remote(sb, rb2, 25, {"tp": t2})
     far_d.start()
-    lax.fori_loop(4 // UNROLL, mid_steps, bwd_body, 0)
+    lax.fori_loop(12 // UNROLL, mid_steps, bwd_body, 0)
 
     keep_dy(0, QR)
     grad_up(0, QR)
@@ -344,7 +345,7 @@
         return jnp.concatenate([dyb[k, 0:QR, :], zs[k * 136 + QR:k * 136 + 64, :].astype(BF16),
                                 dyb[k, 64:64 + QR, :], zs[k * 136 + 64 + QR:k * 136 + 128, :].astype(BF16)], axis=0)
 
-    nsplit = ((0, 9), (9, 16), (16, 25))
+    nsplit = ((0, 6), (6, 16), (16, 25))
     near_n = []
     for j, (k0, k1) in enumerate(nsplit):
         for k, r in by_degree(lambda l: up[l], full_dy, k0, k1):
@@ -373,8 +374,9 @@
     far_step(0)
     keep_dy(QR, half - QR)
     far_send(0)
+    far_step(1)
     grad_up(QR, half - QR)
-    far_step(1)
+    far_send(1)
     far_step(2)
     ex_up1 = remote(gup.at[:, rows_of(odp, QR), :], gup_rb.at[:, QR:64, :], 36, {"dp": odp})
     ex_up1.start()
@@ -386,8 +388,6 @@
             st1 = jnp.sum(rf * hat_s, axis=0, keepdims=True)
         else:
             s3 = s3 + rf * xg[k].astype(F32)
-        if k == 4:
-            far_send(1)
     st2 = jnp.sum(s3, axis=0, keepdims=True)
     st_snd[...] = jnp.concatenate([st0, st1, st2, jnp.zeros((5, nat), F32)], axis=0)
     ex_up0.wait_recv()
@@ -485,7 +485,7 @@
                 pltpu.VMEM((128, nat), BF16),
                 pltpu.VMEM((pp, 256), BF16), pltpu.VMEM((pp, 256), BF16), pltpu.VMEM((pp, 256), BF16), pltpu.VMEM((pp, 256), BF16),
                 pltpu.VMEM((pp, 256), BF16), pltpu.VMEM((pp, 256), BF16), pltpu.VMEM((pp, 256), BF16), pltpu.VMEM((pp, 256), BF16),
-                pltpu.SemaphoreType.DMA((12,)), pltpu.SemaphoreType.DMA((44,)), pltpu.SemaphoreType.DMA((44,)),
+                pltpu.SemaphoreType.DMA((12,)), pltpu.SemaphoreType.DMA((46,)), pltpu.SemaphoreType.DMA((46,)),
             ],
             compiler_params=pltpu.CompilerParams(collective_id=0, has_side_effects=True, vmem_limit_bytes=60 * 1024 * 1024),
         )(xt, gain_loc, up_loc, gate_loc, down_loc, to_grid, from_grid.T, gt)

time: 41.1 us -> 41.3 us (level)
  no operation moved by 1% of the time
where the time goes in v9:
time: 41.3 us; the launch traced here: 41.2 us
  Pallas kernels  40.5 us (98%)
  between operations  0.64 us (2%)
    pallas_call x1, Pallas kernels, local_step(): pl.pallas_call(functools.partial(kernel, tp_size, grid_pts), out_shape=tu...  39.6 us
    pallas_call x1, Pallas kernels, local_step(): pl.pallas_call(flush, out_shape=tuple((jax.ShapeDtypeStruct(sh, BF16) for...  0.91 us

profile of v9, /device:TPU:0, one launch (start us, length us, event | category | flops | bytes accessed | tf_op | source)
XLA Modules:
  0.0 41.2 jit_solution(14601143868618506227)
XLA Ops:
  0.6 39.6 %shard_map.119 = (bf16[25,32,128]{2,1,0:T(8,128)(2,1)S(1)}, bf16[25,32,128]{2,1,0:T(8,128)(2,1)S(1)}, bf16[5,128,128]{2,1,0:T(8,128)(2,1)S(1)}, bf16[128,128]{1,0:T(8,128)(2,1)S(1)}, bf16[5,128,128]{2,1,0:T(8,128)(2,1)S(1)}) custom-call(bf16[25,32,128]{2,1,0:T(8,128)(2,1)} %bitcast.5, f32[5,32]{1,0:T(8,128)} %gain_hbm.1, bf16[5,128,128]{2,1,0:T(8,128)(2,1)} %up_hbm.1, ...), custom_call_target="tpu_custom_call" | custom-call | tf_op jit(solution)/shard_map/pallas_call | solution.py:469
  40.2 0.9 %shard_map.120 = (bf16[25,32,128]{2,1,0:T(8,128)(2,1)}, bf16[25,32,128]{2,1,0:T(8,128)(2,1)}, bf16[5,128,128]{2,1,0:T(8,128)(2,1)}, bf16[128,128]{1,0:T(8,128)(2,1)}, bf16[5,128,128]{2,1,0:T(8,128)(2,1)}) custom-call(bf16[25,32,128]{2,1,0:T(8,128)(2,1)S(1)} %get-tuple-element.15.a, bf16[25,32,128]{2,1,0:T(8,128)(2,1)S(1)} %get-tuple-element.16.b, ...), custom_call_target="tpu_custom_call" | custom-call | tf_op jit(solution)/shard_map/pallas_call | solution.py:492

commit v10 on v9

--- a/solution.py
+++ b/solution.py
@@ -321,12 +321,12 @@
         return pl.ds(pl.multiple_of(d * half + lo, 16), half - QR if lo else QR)
 
     mid_steps = (QR + 4) // UNROLL
-    lax.fori_loop(0, 12 // UNROLL, bwd_body, 0)
+    lax.fori_loop(0, 8 // UNROLL, bwd_body, 0)
     near_d[0].wait_recv()
     sb[...] = (dpart[:, blk(t2), :].astype(F32) + rb1[0].astype(F32)).astype(BF16)
     far_d = remote(sb, rb2, 25, {"tp": t2})
     far_d.start()
-    lax.fori_loop(12 // UNROLL, mid_steps, bwd_body, 0)
+    lax.fori_loop(8 // UNROLL, mid_steps, bwd_body, 0)
 
     keep_dy(0, QR)
     grad_up(0, QR)
@@ -345,7 +345,7 @@
         return jnp.concatenate([dyb[k, 0:QR, :], zs[k * 136 + QR:k * 136 + 64, :].astype(BF16),
                                 dyb[k, 64:64 + QR, :], zs[k * 136 + 64 + QR:k * 136 + 128, :].astype(BF16)], axis=0)
 
-    nsplit = ((0, 6), (6, 16), (16, 25))
+    nsplit = ((0, 9), (9, 16), (16, 25))
     near_n = []
     for j, (k0, k1) in enumerate(nsplit):
         for k, r in by_degree(lambda l: up[l], full_dy, k0, k1):
@@ -374,9 +374,8 @@
     far_step(0)
     keep_dy(QR, half - QR)
     far_send(0)
+    grad_up(QR, half - QR)
     far_step(1)
-    grad_up(QR, half - QR)
-    far_send(1)
     far_step(2)
     ex_up1 = remote(gup.at[:, rows_of(odp, QR), :], gup_rb.at[:, QR:64, :], 36, {"dp": odp})
     ex_up1.start()
@@ -388,6 +387,8 @@
             st1 = jnp.sum(rf * hat_s, axis=0, keepdims=True)
         else:
             s3 = s3 + rf * xg[k].astype(F32)
+        if k == 4:
+            far_send(1)
     st2 = jnp.sum(s3, axis=0, keepdims=True)
     st_snd[...] = jnp.concatenate([st0, st1, st2, jnp.zeros((5, nat), F32)], axis=0)
     ex_up0.wait_recv()
@@ -485,7 +486,7 @@
                 pltpu.VMEM((128, nat), BF16),
                 pltpu.VMEM((pp, 256), BF16), pltpu.VMEM((pp, 256), BF16), pltpu.VMEM((pp, 256), BF16), pltpu.VMEM((pp, 256), BF16),
                 pltpu.VMEM((pp, 256), BF16), pltpu.VMEM((pp, 256), BF16), pltpu.VMEM((pp, 256), BF16), pltpu.VMEM((pp, 256), BF16),
-                pltpu.SemaphoreType.DMA((12,)), pltpu.SemaphoreType.DMA((46,)), pltpu.SemaphoreType.DMA((46,)),
+                pltpu.SemaphoreType.DMA((12,)), pltpu.SemaphoreType.DMA((44,)), pltpu.SemaphoreType.DMA((44,)),
             ],
             compiler_params=pltpu.CompilerParams(collective_id=0, has_side_effects=True, vmem_limit_bytes=60 * 1024 * 1024),
         )(xt, gain_loc, up_loc, gate_loc, down_loc, to_grid, from_grid.T, gt)

time: 41.3 us -> 41.3 us (level)
  no operation moved by 1% of the time
where the time goes in v10:
time: 41.3 us; the launch traced here: 41.2 us
  Pallas kernels  40.5 us (98%)
  between operations  0.64 us (2%)
    pallas_call x1, Pallas kernels, local_step(): pl.pallas_call(functools.partial(kernel, tp_size, grid_pts), out_shape=tu...  39.6 us
    pallas_call x1, Pallas kernels, local_step(): pl.pallas_call(flush, out_shape=tuple((jax.ShapeDtypeStruct(sh, BF16) for...  0.91 us

profile of v10, /device:TPU:0, one launch (start us, length us, event | category | flops | bytes accessed | tf_op | source)
XLA Modules:
  0.0 41.2 jit_solution(3480365572781716526)
XLA Ops:
  0.6 39.6 %shard_map.119 = (bf16[25,32,128]{2,1,0:T(8,128)(2,1)S(1)}, bf16[25,32,128]{2,1,0:T(8,128)(2,1)S(1)}, bf16[5,128,128]{2,1,0:T(8,128)(2,1)S(1)}, bf16[128,128]{1,0:T(8,128)(2,1)S(1)}, bf16[5,128,128]{2,1,0:T(8,128)(2,1)S(1)}) custom-call(bf16[25,32,128]{2,1,0:T(8,128)(2,1)} %bitcast.5, f32[5,32]{1,0:T(8,128)} %gain_hbm.1, bf16[5,128,128]{2,1,0:T(8,128)(2,1)} %up_hbm.1, ...), custom_call_target="tpu_custom_call" | custom-call | tf_op jit(solution)/shard_map/pallas_call | solution.py:470
  40.2 0.9 %shard_map.120 = (bf16[25,32,128]{2,1,0:T(8,128)(2,1)}, bf16[25,32,128]{2,1,0:T(8,128)(2,1)}, bf16[5,128,128]{2,1,0:T(8,128)(2,1)}, bf16[128,128]{1,0:T(8,128)(2,1)}, bf16[5,128,128]{2,1,0:T(8,128)(2,1)}) custom-call(bf16[25,32,128]{2,1,0:T(8,128)(2,1)S(1)} %get-tuple-element.15.a, bf16[25,32,128]{2,1,0:T(8,128)(2,1)S(1)} %get-tuple-element.16.b, ...), custom_call_target="tpu_custom_call" | custom-call | tf_op jit(solution)/shard_map/pallas_call | solution.py:493

commit v11 on v9

--- a/solution.py
+++ b/solution.py
@@ -165,15 +165,15 @@
                 sums[0] = sums[0] + v * v
 
     fwd_x = gather_finish(far_x, near_x, xg, 0, square_step)
+    for c in far_x:
+        c.wait_send()
+    c_g.wait()
+    far_g, near_g = gather_start(gg, 10)
     fwd_x[-1].wait_recv()
     square_step((t2, t3), *ksplit[2])
     far_x[-2].wait_recv()
     far_x[-1].wait_recv()
     square_step((t2, t3), *ksplit[3])
-    for c in far_x:
-        c.wait_send()
-    c_g.wait()
-    far_g, near_g = gather_start(gg, 10)
 
     x0 = xg[0].astype(F32)
     mean_s = jnp.sum(x0, axis=0, keepdims=True) / ch

time: 41.3 us -> 41.2 us (level)
  no operation moved by 1% of the time
where the time goes in v11:
time: 41.2 us; the launch traced here: 41.1 us
  Pallas kernels  40.4 us (98%)
  between operations  0.64 us (2%)
    pallas_call x1, Pallas kernels, local_step(): pl.pallas_call(functools.partial(kernel, tp_size, grid_pts), out_shape=tu...  39.5 us
    pallas_call x1, Pallas kernels, local_step(): pl.pallas_call(flush, out_shape=tuple((jax.ShapeDtypeStruct(sh, BF16) for...  0.91 us

profile of v11, /device:TPU:0, one launch (start us, length us, event | category | flops | bytes accessed | tf_op | source)
XLA Modules:
  0.0 41.1 jit_solution(2095902173898823389)
XLA Ops:
  0.6 39.5 %shard_map.119 = (bf16[25,32,128]{2,1,0:T(8,128)(2,1)S(1)}, bf16[25,32,128]{2,1,0:T(8,128)(2,1)S(1)}, bf16[5,128,128]{2,1,0:T(8,128)(2,1)S(1)}, bf16[128,128]{1,0:T(8,128)(2,1)S(1)}, bf16[5,128,128]{2,1,0:T(8,128)(2,1)S(1)}) custom-call(bf16[25,32,128]{2,1,0:T(8,128)(2,1)} %bitcast.5, f32[5,32]{1,0:T(8,128)} %gain_hbm.1, bf16[5,128,128]{2,1,0:T(8,128)(2,1)} %up_hbm.1, ...), custom_call_target="tpu_custom_call" | custom-call | tf_op jit(solution)/shard_map/pallas_call | solution.py:469
  40.2 0.9 %shard_map.120 = (bf16[25,32,128]{2,1,0:T(8,128)(2,1)}, bf16[25,32,128]{2,1,0:T(8,128)(2,1)}, bf16[5,128,128]{2,1,0:T(8,128)(2,1)}, bf16[128,128]{1,0:T(8,128)(2,1)}, bf16[5,128,128]{2,1,0:T(8,128)(2,1)}) custom-call(bf16[25,32,128]{2,1,0:T(8,128)(2,1)S(1)} %get-tuple-element.15.a, bf16[25,32,128]{2,1,0:T(8,128)(2,1)S(1)} %get-tuple-element.16.b, ...), custom_call_target="tpu_custom_call" | custom-call | tf_op jit(solution)/shard_map/pallas_call | solution.py:492

commit v12 on v8

--- a/solution.py
+++ b/solution.py
@@ -165,15 +165,15 @@
                 sums[0] = sums[0] + v * v
 
     fwd_x = gather_finish(far_x, near_x, xg, 0, square_step)
+    for c in far_x:
+        c.wait_send()
+    c_g.wait()
+    far_g, near_g = gather_start(gg, 10)
     fwd_x[-1].wait_recv()
     square_step((t2, t3), *ksplit[2])
     far_x[-2].wait_recv()
     far_x[-1].wait_recv()
     square_step((t2, t3), *ksplit[3])
-    for c in far_x:
-        c.wait_send()
-    c_g.wait()
-    far_g, near_g = gather_start(gg, 10)
 
     x0 = xg[0].astype(F32)
     mean_s = jnp.sum(x0, axis=0, keepdims=True) / ch

time: 41.1 us -> 41 us (level)
  no operation moved by 1% of the time
where the time goes in v12:
time: 41 us; the launch traced here: 40.9 us
  Pallas kernels  40.3 us (98%)
  between operations  0.64 us (2%)
    pallas_call x1, Pallas kernels, local_step(): pl.pallas_call(functools.partial(kernel, tp_size, grid_pts), out_shape=tu...  39.4 us
    pallas_call x1, Pallas kernels, local_step(): pl.pallas_call(flush, out_shape=tuple((jax.ShapeDtypeStruct(sh, BF16) for...  0.91 us

profile of v12, /device:TPU:0, one launch (start us, length us, event | category | flops | bytes accessed | tf_op | source)
XLA Modules:
  0.0 40.9 jit_solution(17840041526704980333)
XLA Ops:
  0.6 39.4 %shard_map.119 = (bf16[25,32,128]{2,1,0:T(8,128)(2,1)S(1)}, bf16[25,32,128]{2,1,0:T(8,128)(2,1)S(1)}, bf16[5,128,128]{2,1,0:T(8,128)(2,1)S(1)}, bf16[128,128]{1,0:T(8,128)(2,1)S(1)}, bf16[5,128,128]{2,1,0:T(8,128)(2,1)S(1)}) custom-call(bf16[25,32,128]{2,1,0:T(8,128)(2,1)} %bitcast.5, f32[5,32]{1,0:T(8,128)} %gain_hbm.1, bf16[5,128,128]{2,1,0:T(8,128)(2,1)} %up_hbm.1, ...), custom_call_target="tpu_custom_call" | custom-call | tf_op jit(solution)/shard_map/pallas_call | solution.py:469
  40.0 0.9 %shard_map.120 = (bf16[25,32,128]{2,1,0:T(8,128)(2,1)}, bf16[25,32,128]{2,1,0:T(8,128)(2,1)}, bf16[5,128,128]{2,1,0:T(8,128)(2,1)}, bf16[128,128]{1,0:T(8,128)(2,1)}, bf16[5,128,128]{2,1,0:T(8,128)(2,1)}) custom-call(bf16[25,32,128]{2,1,0:T(8,128)(2,1)S(1)} %get-tuple-element.15.a, bf16[25,32,128]{2,1,0:T(8,128)(2,1)S(1)} %get-tuple-element.16.b, ...), custom_call_target="tpu_custom_call" | custom-call | tf_op jit(solution)/shard_map/pallas_call | solution.py:492
